TPU v7x, 128 devices: a whole 4x4x4 slice. The times are simulated.
128 devices in a mesh: batch: 1, graph: 128 (over z, y, x, core).
Axes of the slice: x: 4, y: 4, z: 4, core: 2. Of those that a mesh axis runs over, the one named last changes fastest.
Arguments:
- grid_in: float32 [65536, 267], P(('batch', 'graph'))
- mesh_in: float32 [131072, 3], P(('batch', 'graph'))
- edge_in: float32 [1048576, 4], P(('batch', 'graph'))
- edge_src: int32 [1048576], P(('batch', 'graph'))
- edge_dst: int32 [1048576], P(('batch', 'graph'))
- edge_mask: int32 [1048576], P(('batch', 'graph'))
- grid_w1: bfloat16 [267, 512], replicated
- grid_w2: bfloat16 [512, 512], replicated
- grid_vec: float32 [4, 512], replicated
- mesh_w1: bfloat16 [3, 512], replicated
- mesh_w2: bfloat16 [512, 512], replicated
- mesh_vec: float32 [4, 512], replicated
- embed_w1: bfloat16 [4, 512], replicated
- embed_w2: bfloat16 [512, 512], replicated
- embed_vec: float32 [4, 512], replicated
- edge_w1: bfloat16 [1536, 512], replicated
- edge_w2: bfloat16 [512, 512], replicated
- edge_vec: float32 [4, 512], replicated
- node_w1: bfloat16 [1024, 512], replicated
- node_w2: bfloat16 [512, 512], replicated
- node_vec: float32 [4, 512], replicated
- post_w1: bfloat16 [512, 512], replicated
- post_w2: bfloat16 [512, 512], replicated
- post_vec: float32 [4, 512], replicated
- cot_mesh: bfloat16 [131072, 512], P(('batch', 'graph'))
- cot_grid: bfloat16 [65536, 512], P(('batch', 'graph'))
Outputs:
- output 1: bfloat16 [131072, 512], P(('batch', 'graph'))
- output 2: bfloat16 [65536, 512], P(('batch', 'graph'))
- output 3: float32 [65536, 267], P(('batch', 'graph'))
- output 4: float32 [1536, 512], P(('batch', 'graph'))
- output 5: float32 [512, 512], P(('batch', 'graph'))
All inputs are finite; a program needn't handle non-finite values.
Results may differ from a plain program's by a relative error of at most 0.0100959.
Values are sent between devices in bfloat16 or wider.
A program may use at most 1 GiB of HBM per device.

v0:
```python
import jax
import jax.numpy as jnp
from jax import lax
from jax.sharding import PartitionSpec as P

NORM_EPS = 1e-5


def mlp_forward(x_in, w_one, w_two, vec_rows):
    pre_one = jnp.dot(x_in, w_one, preferred_element_type=jnp.float32) + vec_rows[0]
    act_bf = jax.nn.silu(pre_one).astype(jnp.bfloat16)
    pre_two = jnp.dot(act_bf, w_two, preferred_element_type=jnp.float32) + vec_rows[1]
    centred = pre_two - jnp.mean(pre_two, axis=-1, keepdims=True)
    inv_std = lax.rsqrt(jnp.mean(centred * centred, axis=-1, keepdims=True) + NORM_EPS)
    normed = centred * inv_std
    return normed * vec_rows[2] + vec_rows[3], (pre_one, act_bf, normed, inv_std)


def mlp_backward(d_out, w_two, vec_rows, saved_acts):
    pre_one, act_bf, normed, inv_std = saved_acts
    d_norm = d_out * vec_rows[2]
    d_two = inv_std * (d_norm - jnp.mean(d_norm, axis=-1, keepdims=True)
                       - normed * jnp.mean(d_norm * normed, axis=-1, keepdims=True))
    g_two = d_two.astype(jnp.bfloat16)
    d_act = jnp.einsum('nj,kj->nk', g_two, w_two, preferred_element_type=jnp.float32)
    sig_pre = jax.nn.sigmoid(pre_one)
    d_one = d_act * sig_pre * (1.0 + pre_one * (1.0 - sig_pre))
    return d_one.astype(jnp.bfloat16), g_two


def solution(mesh):
    groups = mesh.shape['graph']
    row_spec = P(('batch', 'graph'), None)
    flat_spec = P(('batch', 'graph'))
    rep_spec = P(None, None)
    down_perm = [(src_dev, src_dev - 1) for src_dev in range(1, groups)]
    up_perm = [(src_dev, src_dev + 1) for src_dev in range(groups - 1)]

    def device_step(grid_in, mesh_in, edge_in, edge_src, edge_dst, edge_mask, grid_w1, grid_w2, grid_vec,
                    mesh_w1, mesh_w2, mesh_vec, embed_w1, embed_w2, embed_vec, edge_w1, edge_w2, edge_vec,
                    node_w1, node_w2, node_vec, post_w1, post_w2, post_vec, cot_mesh, cot_grid):
        band_rows = grid_in.shape[0]
        halo_rows = band_rows // 4
        latent = grid_w2.shape[1]
        mesh_rows = mesh_in.shape[0]
        band_index = lax.axis_index('graph')
        grid_y, grid_saved = mlp_forward(grid_in.astype(jnp.bfloat16), grid_w1, grid_w2, grid_vec)
        grid_h = grid_y.astype(jnp.bfloat16)
        from_above = lax.ppermute(grid_h[:halo_rows], 'graph', down_perm)
        from_below = lax.ppermute(grid_h[band_rows - halo_rows:], 'graph', up_perm)
        row_table = jnp.concatenate([from_below, grid_h, from_above], axis=0)
        local_src = edge_src - (band_index * band_rows - halo_rows)
        mesh_h = mlp_forward(mesh_in.astype(jnp.bfloat16), mesh_w1, mesh_w2, mesh_vec)[0].astype(jnp.bfloat16)
        edge_h = mlp_forward(edge_in.astype(jnp.bfloat16), embed_w1, embed_w2, embed_vec)[0].astype(jnp.bfloat16)
        edge_cat = jnp.concatenate([edge_h, row_table[local_src], mesh_h[edge_dst]], axis=1)
        edge_y, edge_saved = mlp_forward(edge_cat, edge_w1, edge_w2, edge_vec)
        keep_col = edge_mask.astype(jnp.float32)[:, None]
        message = keep_col * (edge_h.astype(jnp.float32) + edge_y)
        agg_sum = jax.ops.segment_sum(message, edge_dst, num_segments=mesh_rows).astype(jnp.bfloat16)
        node_y, node_saved = mlp_forward(jnp.concatenate([mesh_h, agg_sum], axis=1), node_w1, node_w2, node_vec)
        mesh_out = (mesh_h.astype(jnp.float32) + node_y).astype(jnp.bfloat16)
        post_y, post_saved = mlp_forward(grid_h, post_w1, post_w2, post_vec)
        grid_out = (grid_h.astype(jnp.float32) + post_y).astype(jnp.bfloat16)
        node_g1 = mlp_backward(cot_mesh.astype(jnp.float32), node_w2, node_vec, node_saved)[0]
        agg_grad = jnp.einsum('nj,kj->nk', node_g1, node_w1[latent:], preferred_element_type=jnp.float32)
        edge_g1, edge_g2 = mlp_backward(keep_col * agg_grad[edge_dst], edge_w2, edge_vec, edge_saved)
        w1_part = jnp.einsum('ek,ej->kj', edge_cat, edge_g1, preferred_element_type=jnp.float32)
        w2_part = jnp.einsum('ek,ej->kj', edge_saved[1], edge_g2, preferred_element_type=jnp.float32)
        src_grad = jnp.einsum('ej,kj->ek', edge_g1, edge_w1[latent:2 * latent], preferred_element_type=jnp.float32)
        table_grad = jax.ops.segment_sum(src_grad, local_src, num_segments=band_rows + 2 * halo_rows)
        tail_grad = lax.ppermute(table_grad[:halo_rows], 'graph', down_perm)
        head_grad = lax.ppermute(table_grad[band_rows + halo_rows:], 'graph', up_perm)
        edge_part = table_grad[halo_rows:band_rows + halo_rows] + jnp.concatenate(
            [head_grad, jnp.zeros((band_rows - 2 * halo_rows, latent), jnp.float32), tail_grad], axis=0)
        post_g1 = mlp_backward(cot_grid.astype(jnp.float32), post_w2, post_vec, post_saved)[0]
        grid_cot = cot_grid.astype(jnp.float32) + jnp.einsum('nj,kj->nk', post_g1, post_w1,
                                                             preferred_element_type=jnp.float32) + edge_part
        grid_g1 = mlp_backward(grid_cot, grid_w2, grid_vec, grid_saved)[0]
        grid_grad = jnp.einsum('nj,kj->nk', grid_g1, grid_w1, preferred_element_type=jnp.float32)
        w1_grad = lax.psum_scatter(w1_part, 'graph', scatter_dimension=0, tiled=True)
        w2_grad = lax.psum_scatter(w2_part, 'graph', scatter_dimension=0, tiled=True)
        return mesh_out, grid_out, grid_grad, w1_grad, w2_grad

    in_specs = (row_spec, row_spec, row_spec, flat_spec, flat_spec, flat_spec) + (rep_spec,) * 18 + (row_spec, row_spec)
    return jax.shard_map(device_step, mesh=mesh, in_specs=in_specs, out_specs=(row_spec,) * 5, check_vma=False)
```

profile of v0, /device:TPU:1, one launch (start us, length us, event | category | flops | bytes accessed | tf_op | source)
XLA Modules:
  0.0 1093.5 jit_solution(6665978522954421659)
XLA Ops:
  13.7 4.5 collective-permute-start
  20.2 2.3 add_reduce_fusion.3
  27.4 33.8 %gather_fusion.1 = bf16[8192,512]{1,0:T(8,128)(2,1)} fusion(bf16[1024,512]{1,0:T(8,128)(2,1)S(1)} %copy.56, s32[8192]{0:T(1024)S(1)} %fusion.84), kind=kCustom, calls=%fused_computation.1 | custom fusion | bytes 16809984 | tf_op jit(solution)/shard_map/gather | solution.py:55
  61.3 12.0 %copy.58 = bf16[8192,512]{0,1:T(8,128)(2,1)} copy(bf16[8192,512]{1,0:T(8,128)(2,1)} %gather_fusion.1) | data formatting | bytes 16777216 | tf_op jit(solution)/shard_map/gather | solution.py:55
  73.3 12.6 %add_reduce_fusion.1 = (f32[8192]{0:T(1024)S(1)}, f32[8192,512]{0,1:T(8,128)}) fusion(f32[512]{0:T(512)S(1)} %bitcast.57, bf16[512,512]{1,0:T(8,128)(2,1)S(1)} %copy-done.80, bf16[4,512]{1,0:T(4,128)(2,1)S(1)} %copy-done.85, f32[512]{0:T(512)S(1)} %bitcast.98, f32[8192,4]{0,1:T(4,128)S(1)} %copy-done.82), kind=kOutput, calls=%fused_computation.19 | convolution fusion | flops 4362100736 | bytes 17473536 | tf_op jit(solution)/shard_map/dot_general | solution.py:12
  86.0 8.7 multiply_reduce_fusion.2
  97.9 10.6 add_convert_fusion
  111.1 33.6 %gather_fusion = bf16[8192,512]{1,0:T(8,128)(2,1)} fusion(bf16[768,512]{1,0:T(8,128)(2,1)S(1)} %copy.55, s32[8192]{0:T(1024)S(1)} %get-tuple-element.28), kind=kCustom, calls=%fused_computation | custom fusion | bytes 16809984 | tf_op jit(solution)/shard_map/gather | solution.py:55
  144.7 11.6 %copy.57 = bf16[8192,512]{0,1:T(8,128)(2,1)} copy(bf16[8192,512]{1,0:T(8,128)(2,1)} %gather_fusion) | data formatting | bytes 16777216 | tf_op jit(solution)/shard_map/gather | solution.py:55
  156.3 23.0 %multiply_convert_fusion.2 = (bf16[8192,512]{1,0:T(8,128)(2,1)}, f32[8192,512]{1,0:T(8,128)}) fusion(f32[512]{0:T(512)S(1)} %bitcast.91, bf16[1536,512]{1,0:T(8,128)(2,1)S(1)} %copy-done.18, bf16[8192,512]{0,1:T(8,128)(2,1)} %copy.58, bf16[8192,512]{0,1:T(8,128)(2,1)} %copy.57, bf16[8192,512]{0,1:T(8,128)(2,1)} %add_convert_fusion), kind=kOutput, calls=%fused_computation.12 | convolution fusion | flops 12985565184 | bytes 51906560 | tf_op jit(solution)/shard_map/dot_general | solution.py:10
  179.3 11.6 %add_reduce_fusion = (f32[8192]{0:T(1024)S(1)}, f32[8192,512]{0,1:T(8,128)}) fusion(f32[512]{0:T(512)S(1)} %bitcast.49, bf16[8192,512]{1,0:T(8,128)(2,1)} %get-tuple-element.66, bf16[512,512]{1,0:T(8,128)(2,1)S(1)} %copy-done), kind=kOutput, calls=%fused_computation.18 | convolution fusion | flops 4303347712 | bytes 25724928 | tf_op jit(solution)/shard_map/dot_general | solution.py:12
  191.0 8.6 multiply_reduce_fusion.1
  199.6 18.8 %add_multiply_fusion = f32[8192,512]{0,1:T(8,128)} fusion(f32[8192,512]{0,1:T(8,128)} %get-tuple-element.69, f32[512]{0:T(512)S(1)} %bitcast.88, f32[512]{0:T(512)S(1)} %bitcast.54, f32[8192]{0:T(1024)S(1)} %add_rsqrt_fusion, f32[8192]{0:T(1024)S(1)} %broadcast_multiply_fusion.2, f32[512]{0:T(512)S(1)} %bitcast.51, f32[8192]{0:T(1024)S(1)} %convert_element_type.92, ...), kind=kLoop, calls=%fused_computation.10 | loop fusion | flops 58720256 | bytes 50507776 | tf_op jit(solution)/shard_map/mul | solution.py:58
  218.4 17.7 %copy.59 = f32[8192,512]{1,0:T(8,128)} copy(f32[8192,512]{0,1:T(8,128)} %add_multiply_fusion) | data formatting | bytes 33554432 | tf_op jit(solution)/shard_map/mul | solution.py:58
  236.0 49.6 %scatter_custom_fusion = f32[1024,512]{1,0:T(8,128)S(1)} fusion(s32[8192]{0:T(1024)} %param.30, f32[8192,512]{1,0:T(8,128)} %copy.59, f32[]{:T(128)} %constant.52.clone.1), kind=kCustom, calls=%fused_computation.90 | custom fusion | flops 4194304 | bytes 2097664 | tf_op jit(solution)/shard_map/scatter-add | solution.py:59
  287.0 3.1 fusion.4
  290.3 2.7 add_reduce_fusion.2
  293.4 2.3 fusion.8
  295.7 4.8 fusion.11
  300.5 32.7 %gather_fusion.2 = f32[8192,512]{1,0:T(8,128)} fusion(f32[1024,512]{1,0:T(8,128)S(1)} %fusion.11, s32[8192]{0:T(1024)S(1)} %copy-done.16), kind=kCustom, calls=%fused_computation.2 | custom fusion | bytes 33587200 | tf_op jit(solution)/shard_map/gather | solution.py:66
  333.1 17.5 %copy.63 = f32[8192,512]{0,1:T(8,128)} copy(f32[8192,512]{1,0:T(8,128)} %gather_fusion.2) | data formatting | bytes 33554432 | tf_op jit(solution)/shard_map/gather | solution.py:66
  350.6 12.3 %fusion.1 = (f32[8192]{0:T(1024)S(1)}, f32[8192]{0:T(1024)S(1)}) fusion(f32[8192,512]{0,1:T(8,128)} %copy.63, f32[512]{0:T(512)S(1)} %bitcast.55, f32[8192]{0:T(1024)S(1)} %convert_element_type.92, f32[8192]{0:T(1024)S(1)} %add_rsqrt_fusion, f32[8192]{0:T(1024)S(1)} %broadcast_multiply_fusion.2, f32[8192,512]{0,1:T(8,128)} %get-tuple-element.69, ...), kind=kLoop, calls=%fused_computation.20 | loop fusion | flops 33538048 | bytes 33722368 | tf_op jit(solution)/shard_map/reduce_sum | solution.py:22
  362.9 3.1 copy-done.1
  366.0 11.5 %multiply_convert_fusion.1 = bf16[8192,512]{0,1:T(8,128)(2,1)} fusion(f32[8192,512]{0,1:T(8,128)S(1)} %copy-done.1, f32[8192,512]{0,1:T(8,128)} %get-tuple-element.69, f32[8192]{0:T(1024)S(1)} %broadcast_multiply_fusion, f32[8192]{0:T(1024)S(1)} %broadcast_multiply_fusion.1, f32[512]{0:T(512)S(1)} %bitcast.56, f32[8192]{0:T(1024)S(1)} %add_rsqrt_fusion, ...), kind=kLoop, calls=%fused_computation.7 | loop fusion | flops 41943040 | bytes 42110976 | tf_op jit(solution)/shard_map/convert_element_type | solution.py:24
  377.5 15.8 %multiply_convert_fusion = bf16[8192,512]{1,0:T(8,128)(2,1)S(1)} fusion(f32[8192,512]{1,0:T(8,128)} %get-tuple-element.67, bf16[8192,512]{0,1:T(8,128)(2,1)} %multiply_convert_fusion.1, bf16[512,512]{1,0:T(8,128)(2,1)S(1)} %copy-done, f32[512]{0:T(512)S(1)} %bitcast.92), kind=kOutput, calls=%fused_computation.6 | convolution fusion | flops 4336910336 | bytes 34080768 | tf_op jit(solution)/shard_map/nj,kj->nk/dot_general | solution.py:25
  393.3 3.3 copy-done.4
  396.7 18.4 %fusion.2 = f32[1536,512]{1,0:T(8,128)} fusion(bf16[8192,512]{1,0:T(8,128)(2,1)S(1)} %multiply_convert_fusion, bf16[8192,512]{0,1:T(8,128)(2,1)} %copy.58, bf16[8192,512]{0,1:T(8,128)(2,1)} %copy.57, bf16[8192,512]{0,1:T(8,128)(2,1)} %add_convert_fusion), kind=kOutput, calls=%fused_computation.21 | convolution fusion | flops 12960399360 | bytes 36700160 | tf_op jit(solution)/shard_map/ek,ej->kj/dot_general | solution.py:67
  415.1 336.4 %fusion = f32[16,512]{1,0:T(8,128)S(1)} fusion(f32[1536,512]{1,0:T(8,128)} %fusion.2), kind=kCustom, calls=%all-reduce-scatter | all-reduce-scatter fusion | flops 1048577 | bytes 3178496
  765.5 20.4 %collective-permute-start.18 = (f32[16,512]{1,0:T(8,128)S(1)}, f32[16,512]{1,0:T(8,128)S(1)}, u32[]{:S(2)}, u32[]{:S(2)}) collective-permute-start(f32[16,512]{1,0:T(8,128)S(1)} %fusion), channel_id=1, source_target_pairs={{0,15},{1,16},{2,17},{3,18},{4,19},{5,20},{6,21},{7,22},{8,23},{9,... | collective-permute-start | bytes 98312
  785.9 10.5 collective-permute-start.19
  796.5 2.5 collective-permute-start.20
  799.0 5.5 collective-permute-start.21
  804.5 3.4 collective-permute-start.22
  808.0 2.4 fusion.15
  813.7 2.3 collective-permute-start.25
  825.2 2.8 collective-permute-start.30
  831.1 13.9 %fusion.59 = f32[8192,512]{1,0:T(8,128)} fusion(bf16[8192,512]{1,0:T(8,128)(2,1)} %copy-done.4, bf16[1536,512]{1,0:T(8,128)(2,1)} %param.41), kind=kOutput, calls=%fused_computation.104 | convolution fusion | flops 4294967296 | bytes 25690112 | tf_op jit(solution)/shard_map/ej,kj->ek/dot_general | solution.py:69
  845.1 50.3 %scatter_custom_fusion.1 = f32[768,512]{1,0:T(8,128)} fusion(s32[8192]{0:T(1024)} %get-tuple-element.29, f32[8192,512]{1,0:T(8,128)} %fusion.59, f32[]{:T(128)} %constant.52.clone.1), kind=kCustom, calls=%fused_computation.100 | custom fusion | flops 4194304 | bytes 1573376 | tf_op jit(solution)/shard_map/scatter-add | solution.py:70
  903.3 3.4 collective-permute-start.6
  909.5 5.0 collective-permute-start.7
  914.6 3.3 collective-permute-start.8
  922.1 3.0 collective-permute-start.3
  925.1 11.3 %fusion.115 = f32[512,512]{1,0:T(8,128)} fusion(bf16[8192,512]{1,0:T(8,128)(2,1)} %get-tuple-element.66, bf16[8192,512]{0,1:T(8,128)(2,1)} %multiply_convert_fusion.1), kind=kOutput, calls=%fused_computation.170 | convolution fusion | flops 4294967296 | bytes 17825792 | tf_op jit(solution)/shard_map/ek,ej->kj/dot_general | solution.py:68
  937.8 2.3 copy.67
  940.2 14.5 %concatenate.16 = f32[524,512]{1,0:T(8,128)S(1)} concatenate(f32[12,512]{1,0:T(8,128)S(1)} %collective-permute-done.35, f32[16,512]{1,0:T(8,128)} %copy-done.47, f32[16,512]{1,0:T(8,128)} %copy-done.46, f32[16,512]{1,0:T(8,128)} %copy-done.45, f32[16,512]{1,0:T(8,128)} %copy-done.44, f32[16,512]{1,0:T(8,128)} %copy-done.43, f32[16,512]{1,0:T(8,128)} %copy-done.42, ...), dimensions={0} | concatenate | bytes 2146304
  955.4 5.0 fusion.98
  960.4 3.1 fusion.18
  963.5 121.6 %all-reduce.5.cloned.1.call-done = f32[512,512]{1,0:T(8,128)} async-done(((f32[512,512]{1,0:T(8,128)}), f32[512,512]{1,0:T(8,128)}) %all-reduce.5.cloned.1.call-update) | async-done | bytes 1048592
  (290 shorter events, 67.9 us)
Async XLA Ops:
  7.2 172.2 %copy-start = (bf16[512,512]{1,0:T(8,128)(2,1)S(1)}, bf16[512,512]{1,0:T(8,128)(2,1)}, u32[]{:S(2)}) copy-start(bf16[512,512]{1,0:T(8,128)(2,1)} %param.42) | copy-start | bytes 1572868
  7.2 1077.9 %all-reduce.5.cloned.1.call-start = ((), (), s32[]{:S(2)}) async-start(), calls=%async_computation | async-start | bytes 2097152
  13.7 97.0 %collective-permute-start = (bf16[128,512]{0,1:T(8,128)(2,1)}, bf16[128,512]{0,1:T(8,128)(2,1)S(1)}, u32[]{:S(2)}, u32[]{:S(2)}) collective-permute-start(bf16[128,512]{0,1:T(8,128)(2,1)} %get-tuple-element.34), channel_id=1, source_target_pairs={{0,1},{1,2},{2,3},{3,4},{4,5},{5,6},{6,7},{7,8},{8,9},{9,10},{10,1... | collective-permute-start | bytes 393224 | tf_op jit(solution)/shard_map/ppermute | solution.py:50
  18.2 92.5 %collective-permute-start.1 = (bf16[128,512]{0,1:T(8,128)(2,1)}, bf16[128,512]{0,1:T(8,128)(2,1)S(1)}, u32[]{:S(2)}, u32[]{:S(2)}) collective-permute-start(bf16[128,512]{0,1:T(8,128)(2,1)} %get-tuple-element.35), channel_id=1, source_target_pairs={{1,0},{2,1},{3,2},{4,3},{5,4},{6,5},{7,6},{8,7},{9,8},{10,9},{11,1... | collective-permute-start | bytes 393224 | tf_op jit(solution)/shard_map/ppermute | solution.py:49
  22.5 38.7 %copy-start.19 = (f32[1024]{0:T(1024)}, f32[1024]{0:T(1024)S(1)}, u32[]{:S(2)}) copy-start(f32[1024]{0:T(1024)S(1)} %broadcast_multiply_fusion.7) | copy-start | bytes 12292
  396.6 360.1 %copy-start.8 = (f32[512,512]{0,1:T(8,128)S(1)}, f32[512,512]{0,1:T(8,128)}, u32[]{:S(2)}) copy-start(f32[512,512]{0,1:T(8,128)} %get-tuple-element.73) | copy-start | bytes 3145732
  396.6 360.1 %copy-start.61 = (f32[512]{0:T(512)S(1)}, f32[512]{0:T(512)}, u32[]{:S(2)}) copy-start(f32[512]{0:T(512)} %broadcast_multiply_fusion.12) | copy-start | bytes 6148
  396.6 411.3 %copy-start.6 = (f32[512,512]{0,1:T(8,128)S(1)}, f32[512,512]{0,1:T(8,128)}, u32[]{:S(2)}) copy-start(f32[512,512]{0,1:T(8,128)} %copy-done.5) | copy-start | bytes 3145732
  396.6 411.3 %copy-start.52 = (f32[512]{0:T(512)S(1)}, f32[512]{0:T(512)}, u32[]{:S(2)}) copy-start(f32[512]{0:T(512)} %copy-done.51) | copy-start | bytes 6148
  396.6 411.3 %copy-start.59 = (f32[512]{0:T(512)S(1)}, f32[512]{0:T(512)}, u32[]{:S(2)}) copy-start(f32[512]{0:T(512)} %copy-done.58) | copy-start | bytes 6148
  396.7 411.3 %copy-start.64 = (f32[1,512]{1,0:T(1,128)S(1)}, f32[1,512]{1,0:T(1,128)}, u32[]{:S(2)}) copy-start(f32[1,512]{1,0:T(1,128)} %copy-done.63) | copy-start | bytes 6148
  396.7 411.3 %copy-start.67 = (f32[1,512]{1,0:T(1,128)S(1)}, f32[1,512]{1,0:T(1,128)}, u32[]{:S(2)}) copy-start(f32[1,512]{1,0:T(1,128)} %copy-done.66) | copy-start | bytes 6148
  396.7 411.3 %copy-start.72 = (f32[1,512]{1,0:T(1,128)S(1)}, f32[1,512]{1,0:T(1,128)}, u32[]{:S(2)}) copy-start(f32[1,512]{1,0:T(1,128)} %get-tuple-element.36) | copy-start | bytes 6148
  396.7 411.3 %copy-start.74 = (f32[1,512]{1,0:T(1,128)S(1)}, f32[1,512]{1,0:T(1,128)}, u32[]{:S(2)}) copy-start(f32[1,512]{1,0:T(1,128)} %get-tuple-element.39) | copy-start | bytes 6148
  751.5 8.0 collective-permute-start.10
  752.8 8.0 collective-permute-start.11
  754.1 8.0 collective-permute-start.12
  755.4 2.8 collective-permute-start.35
  756.9 8.6 collective-permute-start.13
  758.2 27.7 %collective-permute-start.14 = (f32[16,512]{1,0:T(8,128)S(1)}, f32[16,512]{1,0:T(8,128)S(1)}, u32[]{:S(2)}, u32[]{:S(2)}) collective-permute-start(f32[16,512]{1,0:T(8,128)S(1)} %fusion), channel_id=1, source_target_pairs={{0,11},{1,12},{2,13},{3,14},{4,15},{5,16},{6,17},{7,18},{8,19},{9,... | collective-permute-start | bytes 98312
  759.5 36.9 %collective-permute-start.15 = (f32[16,512]{1,0:T(8,128)S(1)}, f32[16,512]{1,0:T(8,128)S(1)}, u32[]{:S(2)}, u32[]{:S(2)}) collective-permute-start(f32[16,512]{1,0:T(8,128)S(1)} %fusion), channel_id=1, source_target_pairs={{0,12},{1,13},{2,14},{3,15},{4,16},{5,17},{6,18},{7,19},{8,20},{9,... | collective-permute-start | bytes 98312
  760.8 38.2 %collective-permute-start.16 = (f32[16,512]{1,0:T(8,128)S(1)}, f32[16,512]{1,0:T(8,128)S(1)}, u32[]{:S(2)}, u32[]{:S(2)}) collective-permute-start(f32[16,512]{1,0:T(8,128)S(1)} %fusion), channel_id=1, source_target_pairs={{0,13},{1,14},{2,15},{3,16},{4,17},{5,18},{6,19},{7,20},{8,21},{9,... | collective-permute-start | bytes 98312
  762.1 42.4 %collective-permute-start.17 = (f32[16,512]{1,0:T(8,128)S(1)}, f32[16,512]{1,0:T(8,128)S(1)}, u32[]{:S(2)}, u32[]{:S(2)}) collective-permute-start(f32[16,512]{1,0:T(8,128)S(1)} %fusion), channel_id=1, source_target_pairs={{0,14},{1,15},{2,16},{3,17},{4,18},{5,19},{6,20},{7,21},{8,22},{9,... | collective-permute-start | bytes 98312
  765.5 44.9 %collective-permute-start.18 = (f32[16,512]{1,0:T(8,128)S(1)}, f32[16,512]{1,0:T(8,128)S(1)}, u32[]{:S(2)}, u32[]{:S(2)}) collective-permute-start(f32[16,512]{1,0:T(8,128)S(1)} %fusion), channel_id=1, source_target_pairs={{0,15},{1,16},{2,17},{3,18},{4,19},{5,20},{6,21},{7,22},{8,23},{9,... | collective-permute-start | bytes 98312
  785.9 26.1 %collective-permute-start.19 = (f32[16,512]{1,0:T(8,128)S(1)}, f32[16,512]{1,0:T(8,128)S(1)}, u32[]{:S(2)}, u32[]{:S(2)}) collective-permute-start(f32[16,512]{1,0:T(8,128)S(1)} %fusion), channel_id=1, source_target_pairs={{0,16},{1,17},{2,18},{3,19},{4,20},{5,21},{6,22},{7,23},{8,24},{9,... | collective-permute-start | bytes 98312
  796.5 17.2 %collective-permute-start.20 = (f32[16,512]{1,0:T(8,128)S(1)}, f32[16,512]{1,0:T(8,128)S(1)}, u32[]{:S(2)}, u32[]{:S(2)}) collective-permute-start(f32[16,512]{1,0:T(8,128)S(1)} %fusion), channel_id=1, source_target_pairs={{0,17},{1,18},{2,19},{3,20},{4,21},{5,22},{6,23},{7,24},{8,25},{9,... | collective-permute-start | bytes 98312
  799.0 16.9 %collective-permute-start.21 = (f32[16,512]{1,0:T(8,128)S(1)}, f32[16,512]{1,0:T(8,128)S(1)}, u32[]{:S(2)}, u32[]{:S(2)}) collective-permute-start(f32[16,512]{1,0:T(8,128)S(1)} %fusion), channel_id=1, source_target_pairs={{0,18},{1,19},{2,20},{3,21},{4,22},{5,23},{6,24},{7,25},{8,26},{9,... | collective-permute-start | bytes 98312
  804.5 13.1 %collective-permute-start.22 = (f32[16,512]{1,0:T(8,128)S(1)}, f32[16,512]{1,0:T(8,128)S(1)}, u32[]{:S(2)}, u32[]{:S(2)}) collective-permute-start(f32[16,512]{1,0:T(8,128)S(1)} %fusion), channel_id=1, source_target_pairs={{0,19},{1,20},{2,21},{3,22},{4,23},{5,24},{6,25},{7,26},{8,27},{9,... | collective-permute-start | bytes 98312
  810.4 11.5 %collective-permute-start.23 = (f32[16,512]{1,0:T(8,128)S(1)}, f32[16,512]{1,0:T(8,128)S(1)}, u32[]{:S(2)}, u32[]{:S(2)}) collective-permute-start(f32[16,512]{1,0:T(8,128)S(1)} %fusion), channel_id=1, source_target_pairs={{0,20},{1,21},{2,22},{3,23},{4,24},{5,25},{6,26},{7,27},{8,28},{9,... | collective-permute-start | bytes 98312
  812.1 11.4 %collective-permute-start.24 = (f32[16,512]{1,0:T(8,128)S(1)}, f32[16,512]{1,0:T(8,128)S(1)}, u32[]{:S(2)}, u32[]{:S(2)}) collective-permute-start(f32[16,512]{1,0:T(8,128)S(1)} %fusion), channel_id=1, source_target_pairs={{0,21},{1,22},{2,23},{3,24},{4,25},{5,26},{6,27},{7,28},{8,29},{9,... | collective-permute-start | bytes 98312
  813.7 11.5 %collective-permute-start.25 = (f32[16,512]{1,0:T(8,128)S(1)}, f32[16,512]{1,0:T(8,128)S(1)}, u32[]{:S(2)}, u32[]{:S(2)}) collective-permute-start(f32[16,512]{1,0:T(8,128)S(1)} %fusion), channel_id=1, source_target_pairs={{0,22},{1,23},{2,24},{3,25},{4,26},{5,27},{6,28},{7,29},{8,30},{9,... | collective-permute-start | bytes 98312
  816.0 12.0 %collective-permute-start.26 = (f32[16,512]{1,0:T(8,128)S(1)}, f32[16,512]{1,0:T(8,128)S(1)}, u32[]{:S(2)}, u32[]{:S(2)}) collective-permute-start(f32[16,512]{1,0:T(8,128)S(1)} %fusion), channel_id=1, source_target_pairs={{0,23},{1,24},{2,25},{3,26},{4,27},{5,28},{6,29},{7,30},{8,31},{9,... | collective-permute-start | bytes 98312
  817.6 12.1 %collective-permute-start.27 = (f32[16,512]{1,0:T(8,128)S(1)}, f32[16,512]{1,0:T(8,128)S(1)}, u32[]{:S(2)}, u32[]{:S(2)}) collective-permute-start(f32[16,512]{1,0:T(8,128)S(1)} %fusion), channel_id=1, source_target_pairs={{0,24},{1,25},{2,26},{3,27},{4,28},{5,29},{6,30},{7,31},{8,32},{9,... | collective-permute-start | bytes 98312
  821.9 73.6 %collective-permute-start.28 = (f32[16,512]{1,0:T(8,128)S(1)}, f32[16,512]{1,0:T(8,128)S(1)}, u32[]{:S(2)}, u32[]{:S(2)}) collective-permute-start(f32[16,512]{1,0:T(8,128)S(1)} %fusion), channel_id=1, source_target_pairs={{0,25},{1,26},{2,27},{3,28},{4,29},{5,30},{6,31},{7,32},{8,33},{9,... | collective-permute-start | bytes 98312
  823.5 73.3 %collective-permute-start.29 = (f32[16,512]{1,0:T(8,128)S(1)}, f32[16,512]{1,0:T(8,128)S(1)}, u32[]{:S(2)}, u32[]{:S(2)}) collective-permute-start(f32[16,512]{1,0:T(8,128)S(1)} %fusion), channel_id=1, source_target_pairs={{0,26},{1,27},{2,28},{3,29},{4,30},{5,31},{6,32},{7,33},{8,34},{9,... | collective-permute-start | bytes 98312
  825.2 73.0 %collective-permute-start.30 = (f32[16,512]{1,0:T(8,128)S(1)}, f32[16,512]{1,0:T(8,128)S(1)}, u32[]{:S(2)}, u32[]{:S(2)}) collective-permute-start(f32[16,512]{1,0:T(8,128)S(1)} %fusion), channel_id=1, source_target_pairs={{0,27},{1,28},{2,29},{3,30},{4,31},{5,32},{6,33},{7,34},{8,35},{9,... | collective-permute-start | bytes 98312
  828.0 72.4 %collective-permute-start.31 = (f32[16,512]{1,0:T(8,128)S(1)}, f32[16,512]{1,0:T(8,128)S(1)}, u32[]{:S(2)}, u32[]{:S(2)}) collective-permute-start(f32[16,512]{1,0:T(8,128)S(1)} %fusion), channel_id=1, source_target_pairs={{0,28},{1,29},{2,30},{3,31},{4,32},{5,33},{6,34},{7,35},{8,36},{9,... | collective-permute-start | bytes 98312
  829.7 72.9 %collective-permute-start.32 = (f32[16,512]{1,0:T(8,128)S(1)}, f32[16,512]{1,0:T(8,128)S(1)}, u32[]{:S(2)}, u32[]{:S(2)}) collective-permute-start(f32[16,512]{1,0:T(8,128)S(1)} %fusion), channel_id=1, source_target_pairs={{0,29},{1,30},{2,31},{3,32},{4,33},{5,34},{6,35},{7,36},{8,37},{9,... | collective-permute-start | bytes 98312
  895.4 14.1 %collective-permute-start.33 = (f32[16,512]{1,0:T(8,128)S(1)}, f32[16,512]{1,0:T(8,128)S(1)}, u32[]{:S(2)}, u32[]{:S(2)}) collective-permute-start(f32[16,512]{1,0:T(8,128)S(1)} %fusion), channel_id=1, source_target_pairs={{0,30},{1,31},{2,32},{3,33},{4,34},{5,35},{6,36},{7,37},{8,38},{9,... | collective-permute-start | bytes 98312
  896.8 17.8 %collective-permute-start.34 = (f32[16,512]{1,0:T(8,128)S(1)}, f32[16,512]{1,0:T(8,128)S(1)}, u32[]{:S(2)}, u32[]{:S(2)}) collective-permute-start(f32[16,512]{1,0:T(8,128)S(1)} %fusion), channel_id=1, source_target_pairs={{0,31},{1,32},{2,33},{3,34},{4,35},{5,36},{6,37},{7,38},{8,39},{9,... | collective-permute-start | bytes 98312
  898.2 19.8 %collective-permute-start.4 = (f32[16,512]{1,0:T(8,128)S(1)}, f32[16,512]{1,0:T(8,128)S(1)}, u32[]{:S(2)}, u32[]{:S(2)}) collective-permute-start(f32[16,512]{1,0:T(8,128)S(1)} %fusion), channel_id=1, source_target_pairs={{0,1},{1,2},{2,3},{3,4},{4,5},{5,6},{6,7},{7,8},{8,9},{9,10},{10,1... | collective-permute-start | bytes 98312
  900.4 19.4 %collective-permute-start.5 = (f32[16,512]{1,0:T(8,128)S(1)}, f32[16,512]{1,0:T(8,128)S(1)}, u32[]{:S(2)}, u32[]{:S(2)}) collective-permute-start(f32[16,512]{1,0:T(8,128)S(1)} %fusion), channel_id=1, source_target_pairs={{0,2},{1,3},{2,4},{3,5},{4,6},{5,7},{6,8},{7,9},{8,10},{9,11},{10,... | collective-permute-start | bytes 98312
  903.3 18.8 %collective-permute-start.6 = (f32[16,512]{1,0:T(8,128)S(1)}, f32[16,512]{1,0:T(8,128)S(1)}, u32[]{:S(2)}, u32[]{:S(2)}) collective-permute-start(f32[16,512]{1,0:T(8,128)S(1)} %fusion), channel_id=1, source_target_pairs={{0,3},{1,4},{2,5},{3,6},{4,7},{5,8},{6,9},{7,10},{8,11},{9,12},{10... | collective-permute-start | bytes 98312
  909.5 30.6 %collective-permute-start.7 = (f32[16,512]{1,0:T(8,128)S(1)}, f32[16,512]{1,0:T(8,128)}, u32[]{:S(2)}, u32[]{:S(2)}) collective-permute-start(f32[16,512]{1,0:T(8,128)S(1)} %fusion), channel_id=1, source_target_pairs={{0,4},{1,5},{2,6},{3,7},{4,8},{5,9},{6,10},{7,11},{8,12},{9,13},{1... | collective-permute-start | bytes 98312
  914.6 25.5 %collective-permute-start.8 = (f32[16,512]{1,0:T(8,128)S(1)}, f32[16,512]{1,0:T(8,128)}, u32[]{:S(2)}, u32[]{:S(2)}) collective-permute-start(f32[16,512]{1,0:T(8,128)S(1)} %fusion), channel_id=1, source_target_pairs={{0,5},{1,6},{2,7},{3,8},{4,9},{5,10},{6,11},{7,12},{8,13},{9,14},{... | collective-permute-start | bytes 98312
  917.9 22.2 %collective-permute-start.9 = (f32[16,512]{1,0:T(8,128)S(1)}, f32[16,512]{1,0:T(8,128)}, u32[]{:S(2)}, u32[]{:S(2)}) collective-permute-start(f32[16,512]{1,0:T(8,128)S(1)} %fusion), channel_id=1, source_target_pairs={{0,6},{1,7},{2,8},{3,9},{4,10},{5,11},{6,12},{7,13},{8,14},{9,15},... | collective-permute-start | bytes 98312
  919.8 35.5 %collective-permute-start.2 = (f32[128,512]{0,1:T(8,128)}, f32[128,512]{0,1:T(8,128)}, u32[]{:S(2)}, u32[]{:S(2)}) collective-permute-start(f32[128,512]{0,1:T(8,128)} %copy.70), channel_id=1, source_target_pairs={{0,1},{1,2},{2,3},{3,4},{4,5},{5,6},{6,7},{7,8},{8,9},{9,10},{10,1... | collective-permute-start | bytes 786440 | tf_op jit(solution)/shard_map/ppermute | solution.py:72
  922.1 33.3 %collective-permute-start.3 = (f32[128,512]{0,1:T(8,128)}, f32[128,512]{0,1:T(8,128)}, u32[]{:S(2)}, u32[]{:S(2)}) collective-permute-start(f32[128,512]{0,1:T(8,128)} %copy.71), channel_id=1, source_target_pairs={{1,0},{2,1},{3,2},{4,3},{5,4},{6,5},{7,6},{8,7},{9,8},{10,9},{11,1... | collective-permute-start | bytes 786440 | tf_op jit(solution)/shard_map/ppermute | solution.py:71
  (77 other events, 1125.5 us)
Sparse Core Ops, SparseCore 0:
  936.6 148.4 all-reduce.4
where the time goes:
time: 1100 us; the launch traced here: 1090 us
  blocking collectives  336 us (31%)
  local copies, waits for them, and re-layouts  202 us (18%)
  other arithmetic  180 us (16%)
  matrix products  133 us (12%)
  waiting for transfers between devices  122 us (11%)
  starting transfers between devices  104 us (9%)
  between operations  16.1 us (1%)
    unnamed x1, blocking collectives  336 us
    unnamed x34, waiting for transfers between devices  122 us
    unnamed x33, starting transfers between devices  92.6 us
    scatter-add x1, other arithmetic, device_step(): jax.ops.segment_sum(src_grad, local_src, num_segments=band_rows + 2 * hal...  50.3 us
    gather x2, local copies, waits for them, and re-layouts, device_step(): agg_grad[edge_dst]  50.1 us
    scatter-add x1, other arithmetic, device_step(): jax.ops.segment_sum(message, edge_dst, num_segments=mesh_rows)  49.6 us
    gather x2, local copies, waits for them, and re-layouts, device_step(): mesh_h[edge_dst]  45.8 us
    gather x2, local copies, waits for them, and re-layouts, device_step(): row_table[local_src]  45.2 us
  transfers between devices with their start and end apart: 37, of which 1 were waited for; matrix products, arithmetic and copies ran while one was open for 18% of the time, Pallas kernels for 0%

commit v1 on v0

v1 whole, which is shorter than its diff:
```python
import functools

import jax
import jax.numpy as jnp
from jax import lax
from jax.experimental import pallas as pl
from jax.experimental.pallas import tpu as pltpu
from jax.sharding import PartitionSpec as P

NORM_EPS = 1e-5
LANES = 128
SUB = 256
STEP = 1024
BF = jnp.bfloat16
F32 = jnp.float32


def mm(lhs, rhs):
    return jnp.dot(lhs, rhs, preferred_element_type=F32)


def mm_t(lhs, rhs):
    return lax.dot_general(lhs, rhs, (((1,), (1,)), ((), ())), preferred_element_type=F32)


def split3(val):
    hi = val.astype(BF)
    rest = val - hi.astype(F32)
    mid = rest.astype(BF)
    lo = (rest - mid.astype(F32)).astype(BF)
    return hi, mid, lo


def sigmoid(val):
    return 0.5 * jnp.tanh(0.5 * val) + 0.5


def lanes_of(col, width):
    return jnp.concatenate([col] * (width // LANES), axis=1)


def one_hot(ids_row, first, rows):
    row_ids = lax.broadcasted_iota(jnp.int32, (rows, ids_row.shape[1]), 0) + first
    return jnp.where(row_ids == ids_row, 1.0, 0.0).astype(BF)


def norm_fwd(val):
    centred = val - jnp.mean(val, axis=0, keepdims=True)
    inv = lax.rsqrt(jnp.mean(centred * centred, axis=0, keepdims=True) + NORM_EPS)
    return centred * inv, inv


def edge_fwd_kernel(mesh_tiles, table_rows, tile_ref, fit_ref, live_ref, feat_ref, key_ref, em_w1t, em_w2t, em_vec,
                    w1t, w2t, vec, table_t, hm_t, he_out, pre_out, norm_out, inv_out, agg_out):
    step = pl.program_id(0)
    latent = w2t.shape[0]
    shift = 10

    @pl.when(step == 0)
    def _():
        agg_out[...] = jnp.zeros_like(agg_out)

    def body(whole):
        for sub in range(STEP // SUB):
            cols = pl.ds(sub * SUB, SUB)
            vec_at = lambda ref, row: lanes_of(ref[row], SUB)
            key = key_ref[:, cols]
            src = key & (2 ** shift - 1)
            dst = key >> shift
            feat = feat_ref[:, cols].astype(BF)
            pre = mm(em_w1t[...], feat) + vec_at(em_vec, 0)
            act = (pre * sigmoid(pre)).astype(BF)
            normed, _ = norm_fwd(mm(em_w2t[...], act) + vec_at(em_vec, 1))
            he = (normed * vec_at(em_vec, 2) + vec_at(em_vec, 3)).astype(BF)
            he_out[:, cols] = he
            hg = mm(table_t[...], one_hot(src, 0, table_rows)).astype(BF)
            if whole:
                tiles = list(range(mesh_tiles))
                hot = one_hot(dst, 0, mesh_tiles * LANES)
            else:
                first = tile_ref[step * (STEP // SUB) + sub]
                tiles = [first, first + 1]
                hot = one_hot(dst, first * LANES, 2 * LANES)
            window = jnp.concatenate([hm_t[t] for t in tiles], axis=1)
            hm = mm(window, hot).astype(BF)
            pre = mm(w1t[:, :latent], he) + mm(w1t[:, latent:2 * latent], hg) + mm(w1t[:, 2 * latent:], hm)
            pre = pre + vec_at(vec, 0)
            pre_out[:, cols] = pre
            act = (pre * sigmoid(pre)).astype(BF)
            normed, inv = norm_fwd(mm(w2t[...], act) + vec_at(vec, 1))
            norm_out[:, cols] = normed
            inv_out[:, cols] = inv
            msg = he.astype(F32) + (normed * vec_at(vec, 2) + vec_at(vec, 3))
            hi, mid, lo = split3(msg)
            add = mm_t(hi, hot) + mm_t(mid, hot) + mm_t(lo, hot)
            for idx, tile in enumerate(tiles):
                agg_out[tile] += add[:, idx * LANES:(idx + 1) * LANES]

    live = step * STEP < live_ref[0]
    fit = fit_ref[step] == 1

    @pl.when(live & fit)
    def _():
        body(False)

    @pl.when(live & jnp.logical_not(fit))
    def _():
        body(True)


def edge_bwd_kernel(mesh_tiles, table_rows, steps, tile_ref, fit_ref, live_ref, key_ref, he_ref, pre_ref, norm_ref, inv_ref,
                    node_wb, w1b, w2, vec, table_t, both_t, w1_out, w2_out, table_out,
                    g1_buf, g2_buf, act_buf, hm_buf, hot_buf, sum_buf):
    step = pl.program_id(0)
    latent = w2.shape[0]
    shift = 10

    @pl.when(step == 0)
    def _():
        w1_out[...] = jnp.zeros_like(w1_out)
        w2_out[...] = jnp.zeros_like(w2_out)
        sum_buf[...] = jnp.zeros_like(sum_buf)

    def body(whole):
        for sub in range(STEP // SUB):
            cols = pl.ds(sub * SUB, SUB)
            key = key_ref[:, cols]
            src = key & (2 ** shift - 1)
            dst = key >> shift
            if whole:
                tiles = list(range(mesh_tiles))
                hot = one_hot(dst, 0, mesh_tiles * LANES)
            else:
                first = tile_ref[step * (STEP // SUB) + sub]
                tiles = [first, first + 1]
                hot = one_hot(dst, first * LANES, 2 * LANES)
            window = jnp.concatenate([both_t[t] for t in tiles], axis=1)
            both = mm(window, hot).astype(BF)
            hm_buf[:, cols] = both[:latent]
            hot_buf[:, cols] = one_hot(src, 0, table_rows)
            d_norm = mm(node_wb[...], both[latent:]) * lanes_of(vec[2], SUB)
            normed = norm_ref[:, cols]
            d_two = inv_ref[:, cols] * (d_norm - jnp.mean(d_norm, axis=0, keepdims=True)
                                        - normed * jnp.mean(d_norm * normed, axis=0, keepdims=True))
            g_two = d_two.astype(BF)
            g2_buf[:, cols] = g_two
            d_act = mm(w2[...], g_two)
            pre = pre_ref[:, cols]
            sig = sigmoid(pre)
            g1_buf[:, cols] = (d_act * sig * (1.0 + pre * (1.0 - sig))).astype(BF)
            act_buf[:, cols] = (pre * sig).astype(BF)
        w2_out[...] += mm_t(act_buf[...], g2_buf[...])
        g_one = g1_buf[...]
        w1_out[:latent] += mm_t(he_ref[...], g_one)
        w1_out[2 * latent:] += mm_t(hm_buf[...], g_one)
        sum_buf[...] += mm_t(hot_buf[...], g_one)

    live = step * STEP < live_ref[0]
    fit = fit_ref[step] == 1

    @pl.when(live & fit)
    def _():
        body(False)

    @pl.when(live & jnp.logical_not(fit))
    def _():
        body(True)

    @pl.when(step == steps - 1)
    def _():
        hi, mid, lo = split3(sum_buf[...])
        w1_out[latent:2 * latent] = mm(table_t[...], hi) + mm(table_t[...], mid) + mm(table_t[...], lo)
        table_out[...] = mm_t(hi, w1b[...]) + mm_t(mid, w1b[...]) + mm_t(lo, w1b[...])


def mlp_forward(x_in, w_one, w_two, vec_rows):
    pre_one = jnp.dot(x_in, w_one, preferred_element_type=jnp.float32) + vec_rows[0]
    act_bf = jax.nn.silu(pre_one).astype(jnp.bfloat16)
    pre_two = jnp.dot(act_bf, w_two, preferred_element_type=jnp.float32) + vec_rows[1]
    centred = pre_two - jnp.mean(pre_two, axis=-1, keepdims=True)
    inv_std = lax.rsqrt(jnp.mean(centred * centred, axis=-1, keepdims=True) + NORM_EPS)
    normed = centred * inv_std
    return normed * vec_rows[2] + vec_rows[3], (pre_one, act_bf, normed, inv_std)


def mlp_backward(d_out, w_two, vec_rows, saved_acts):
    pre_one, act_bf, normed, inv_std = saved_acts
    d_norm = d_out * vec_rows[2]
    d_two = inv_std * (d_norm - jnp.mean(d_norm, axis=-1, keepdims=True)
                       - normed * jnp.mean(d_norm * normed, axis=-1, keepdims=True))
    g_two = d_two.astype(jnp.bfloat16)
    d_act = jnp.einsum('nj,kj->nk', g_two, w_two, preferred_element_type=jnp.float32)
    sig_pre = jax.nn.sigmoid(pre_one)
    d_one = d_act * sig_pre * (1.0 + pre_one * (1.0 - sig_pre))
    return d_one.astype(jnp.bfloat16), g_two


def whole_spec(arr):
    zeros = (0,) * arr.ndim
    return pl.BlockSpec(arr.shape, lambda i, *_: zeros)


def lane_table(vec_rows):
    return jnp.broadcast_to(vec_rows[:, :, None], vec_rows.shape + (LANES,))


def feature_major(rows):
    return jnp.swapaxes(rows.reshape(-1, LANES, rows.shape[1]), 1, 2)


def solution(mesh):
    groups = mesh.shape['graph']
    row_spec = P(('batch', 'graph'), None)
    flat_spec = P(('batch', 'graph'))
    rep_spec = P(None, None)
    down_perm = [(src_dev, src_dev - 1) for src_dev in range(1, groups)]
    up_perm = [(src_dev, src_dev + 1) for src_dev in range(groups - 1)]

    def device_step(grid_in, mesh_in, edge_in, edge_src, edge_dst, edge_mask, grid_w1, grid_w2, grid_vec,
                    mesh_w1, mesh_w2, mesh_vec, embed_w1, embed_w2, embed_vec, edge_w1, edge_w2, edge_vec,
                    node_w1, node_w2, node_vec, post_w1, post_w2, post_vec, cot_mesh, cot_grid):
        band_rows = grid_in.shape[0]
        halo_rows = band_rows // 4
        latent = grid_w2.shape[1]
        mesh_rows = mesh_in.shape[0]
        edges = edge_in.shape[0]
        table_rows = band_rows + 2 * halo_rows
        mesh_tiles = mesh_rows // LANES
        steps = edges // STEP
        band_index = lax.axis_index('graph')

        grid_y, grid_saved = mlp_forward(grid_in.astype(BF), grid_w1, grid_w2, grid_vec)
        grid_h = grid_y.astype(BF)
        from_above = lax.ppermute(grid_h[:halo_rows], 'graph', down_perm)
        from_below = lax.ppermute(grid_h[band_rows - halo_rows:], 'graph', up_perm)

        local_src = edge_src - (band_index * band_rows - halo_rows)
        real = edge_mask != 0
        key = jnp.where(real, edge_dst * 1024 + local_src, mesh_rows * 1024)
        feat_t = edge_in.T
        key, f0, f1, f2, f3 = lax.sort((key, feat_t[0], feat_t[1], feat_t[2], feat_t[3]), num_keys=1, is_stable=False)
        zero_row = jnp.zeros_like(f0)
        feats = jnp.stack([f0, f1, f2, f3, zero_row, zero_row, zero_row, zero_row])
        live = jnp.sum(real.astype(jnp.int32)).reshape(1)
        dst_sorted = (key >> 10).reshape(-1, SUB)
        low = jnp.min(dst_sorted, axis=1)
        high = jnp.max(jnp.where(dst_sorted < mesh_rows, dst_sorted, 0), axis=1)
        first_tile = jnp.minimum(low // LANES, mesh_tiles - 2)
        fits = ((high - first_tile * LANES) < 2 * LANES).reshape(steps, STEP // SUB)
        fits = jnp.all(fits, axis=1).astype(jnp.int32)
        key_row = key.reshape(1, edges)

        mesh_h = mlp_forward(mesh_in.astype(BF), mesh_w1, mesh_w2, mesh_vec)[0].astype(BF)
        table_t = jnp.concatenate([from_below, grid_h, from_above], axis=0).T
        hm_t = feature_major(mesh_h)
        em_w1t = jnp.pad(embed_w1, ((0, 8 - embed_w1.shape[0]), (0, 0))).T
        edge_vec_t = lane_table(edge_vec)

        lane_block = lambda rows: pl.BlockSpec((rows, STEP), lambda i, *_: (0, i))
        fwd_in = (feats, key_row, em_w1t, embed_w2.T, lane_table(embed_vec), edge_w1.T, edge_w2.T, edge_vec_t, table_t, hm_t)
        he_t, pre_t, norm_t, inv_t, agg_t = pl.pallas_call(
            functools.partial(edge_fwd_kernel, mesh_tiles, table_rows),
            grid_spec=pltpu.PrefetchScalarGridSpec(
                num_scalar_prefetch=3, grid=(steps,),
                in_specs=[lane_block(8), lane_block(1)] + [whole_spec(a) for a in fwd_in[2:]],
                out_specs=[lane_block(latent), lane_block(latent), lane_block(latent), lane_block(1),
                           pl.BlockSpec((mesh_tiles, latent, LANES), lambda i, *_: (0, 0, 0))]),
            out_shape=[jax.ShapeDtypeStruct((latent, edges), BF), jax.ShapeDtypeStruct((latent, edges), F32),
                       jax.ShapeDtypeStruct((latent, edges), F32), jax.ShapeDtypeStruct((1, edges), F32),
                       jax.ShapeDtypeStruct((mesh_tiles, latent, LANES), F32)],
            compiler_params=pltpu.CompilerParams(dimension_semantics=("arbitrary",), vmem_limit_bytes=60 * 2 ** 20),
            cost_estimate=pl.CostEstimate(flops=9 * 2 * edges * latent * latent, bytes_accessed=64 * 2 ** 20,
                                          transcendentals=2 * edges * latent),
            name="edge_fwd",
        )(first_tile, fits, live, *fwd_in)

        agg_sum = jnp.swapaxes(agg_t, 1, 2).reshape(mesh_rows, latent).astype(BF)
        node_y, node_saved = mlp_forward(jnp.concatenate([mesh_h, agg_sum], axis=1), node_w1, node_w2, node_vec)
        mesh_out = (mesh_h.astype(F32) + node_y).astype(BF)
        node_g1 = mlp_backward(cot_mesh.astype(F32), node_w2, node_vec, node_saved)[0]

        both_t = jnp.concatenate([hm_t, feature_major(node_g1)], axis=1)
        w1b = edge_w1[latent:2 * latent]
        bwd_in = (key_row, he_t, pre_t, norm_t, inv_t, node_w1[latent:], w1b, edge_w2, edge_vec_t, table_t, both_t)
        w1_part, w2_part, table_grad = pl.pallas_call(
            functools.partial(edge_bwd_kernel, mesh_tiles, table_rows, steps),
            grid_spec=pltpu.PrefetchScalarGridSpec(
                num_scalar_prefetch=3, grid=(steps,),
                in_specs=[lane_block(1), lane_block(latent), lane_block(latent), lane_block(latent), lane_block(1)]
                + [whole_spec(a) for a in bwd_in[5:]],
                out_specs=[pl.BlockSpec((3 * latent, latent), lambda i, *_: (0, 0)),
                           pl.BlockSpec((latent, latent), lambda i, *_: (0, 0)),
                           pl.BlockSpec((table_rows, latent), lambda i, *_: (0, 0))],
                scratch_shapes=[pltpu.VMEM((latent, STEP), BF)] * 4
                + [pltpu.VMEM((table_rows, STEP), BF), pltpu.VMEM((table_rows, latent), F32)]),
            out_shape=[jax.ShapeDtypeStruct((3 * latent, latent), F32), jax.ShapeDtypeStruct((latent, latent), F32),
                       jax.ShapeDtypeStruct((table_rows, latent), F32)],
            compiler_params=pltpu.CompilerParams(dimension_semantics=("arbitrary",), vmem_limit_bytes=60 * 2 ** 20),
            cost_estimate=pl.CostEstimate(flops=15 * edges * latent * latent, bytes_accessed=64 * 2 ** 20,
                                          transcendentals=edges * latent),
            name="edge_bwd",
        )(first_tile, fits, live, *bwd_in)

        w_parts = jnp.concatenate([w1_part.reshape(groups, -1, latent), w2_part.reshape(groups, -1, latent)], axis=1)
        w_sum = lax.psum_scatter(w_parts, 'graph', scatter_dimension=0, tiled=True)[0]
        w1_grad, w2_grad = w_sum[:w1_part.shape[0] // groups], w_sum[w1_part.shape[0] // groups:]

        tail_grad = lax.ppermute(table_grad[:halo_rows], 'graph', down_perm)
        head_grad = lax.ppermute(table_grad[band_rows + halo_rows:], 'graph', up_perm)
        post_y, post_saved = mlp_forward(grid_h, post_w1, post_w2, post_vec)
        grid_out = (grid_h.astype(F32) + post_y).astype(BF)
        post_g1 = mlp_backward(cot_grid.astype(F32), post_w2, post_vec, post_saved)[0]
        grid_cot = cot_grid.astype(F32) + jnp.einsum('nj,kj->nk', post_g1, post_w1, preferred_element_type=F32)
        edge_part = table_grad[halo_rows:band_rows + halo_rows] + jnp.concatenate(
            [head_grad, jnp.zeros((band_rows - 2 * halo_rows, latent), F32), tail_grad], axis=0)
        grid_g1 = mlp_backward(grid_cot + edge_part, grid_w2, grid_vec, grid_saved)[0]
        grid_grad = jnp.einsum('nj,kj->nk', grid_g1, grid_w1, preferred_element_type=F32)
        return mesh_out, grid_out, grid_grad, w1_grad, w2_grad

    in_specs = (row_spec, row_spec, row_spec, flat_spec, flat_spec, flat_spec) + (rep_spec,) * 18 + (row_spec, row_spec)
    return jax.shard_map(device_step, mesh=mesh, in_specs=in_specs, out_specs=(row_spec,) * 5, check_vma=False)
```

time: 1100 us -> 913 us (0.83)
  waiting for transfers between devices: 122 us -> 665 us
  blocking collectives: 336 us -> 0 us
  local copies, waits for them, and re-layouts: 202 us -> 41.7 us
  other arithmetic: 180 us -> 25.7 us
  Pallas kernels: 0 us -> 125 us
  matrix products: 133 us -> 21.2 us
  starting transfers between devices: 104 us -> 12 us
    reduce_scatter x0 -> x1, waiting for transfers between devices: none -> 621 us  [device_step(): lax.psum_scatter(w_parts, 'graph', scatter_dimension=0, tiled=True)[0]]
    unnamed x1 -> x0, blocking collectives: 336 us -> none
    gather x6 -> x0, local copies, waits for them, and re-layouts: 141 us -> none  [the longest x2 50.1 us: device_step(): agg_grad[edge_dst]]
    pallas_call x0 -> x2, Pallas kernels: none -> 125 us  [the longest x1 77.9 us: device_step(): pl.pallas_call(functools.partial(edge_fwd_kernel, mesh_tiles, table_rows)...]
    unnamed x34 -> x1, waiting for transfers between devices: 122 us -> 0.02 us
    scatter-add x2 -> x0, other arithmetic: 99.9 us -> none  [the longest x1 50.3 us: device_step(): jax.ops.segment_sum(src_grad, local_src, num_segments=band_rows + 2 * hal...]
    unnamed x33 -> x0, starting transfers between devices: 92.6 us -> none
    dot_general x6 -> x2, matrix products: 56.4 us -> 7.66 us  [the longest x1 4.21 us: device_step(): jnp.einsum('nj,kj->nk', post_g1, post_w1, preferred_element_type=F32)]
  transfers between devices with their start and end apart: 37 -> 5, of which waited for: 1 -> 2; matrix products, arithmetic and copies ran while one was open for 18% -> 5% of each run, Pallas kernels for 0% -> 0%
where the time goes in v1:
time: 913 us; the launch traced here: 905 us
  waiting for transfers between devices  665 us (73%)
  Pallas kernels  125 us (14%)
  local copies, waits for them, and re-layouts  41.7 us (5%)
  other arithmetic  25.7 us (3%)
  matrix products  21.2 us (2%)
  between operations  14.9 us (2%)
  starting transfers between devices  12 us (1%)
    reduce_scatter x1, waiting for transfers between devices, device_step(): lax.psum_scatter(w_parts, 'graph', scatter_dimension=0, tiled=True)[0]  621 us
    pallas_call x1, Pallas kernels, device_step(): pl.pallas_call(functools.partial(edge_fwd_kernel, mesh_tiles, table_rows)...  77.9 us
    pallas_call x1, Pallas kernels, device_step(): pl.pallas_call(functools.partial(edge_bwd_kernel, mesh_tiles, table_rows,...  46.7 us
    ppermute x1, waiting for transfers between devices, device_step(): tail_grad = lax.ppermute(table_grad[:halo_rows], 'graph', down_perm)  43.9 us
  transfers between devices with their start and end apart: 5, of which 2 were waited for; matrix products, arithmetic and copies ran while one was open for 5% of the time, Pallas kernels for 0%

profile of v1, /device:TPU:1, one launch (start us, length us, event | category | flops | bytes accessed | tf_op | source)
XLA Modules:
  0.0 904.7 jit_solution(2005521338239836975)
XLA Ops:
  7.2 0.9 fusion.84
  8.1 1.6 convolution_add_fusion.4
  9.7 2.0 fusion.86
  12.0 0.7 copy-done.2
  12.9 0.7 fusion.80
  13.6 4.5 collective-permute-start
  18.1 1.9 collective-permute-start.1
  20.2 0.7 convert_reduce_fusion
  20.9 6.5 sort.33
  28.3 2.3 add_reduce_fusion.1
  31.9 1.4 add_convert_fusion.1
  33.5 2.6 copy.56
  36.0 1.9 slice.119.w1b
  37.9 2.3 copy.58
  40.2 0.6 convert_element_type.82.fit_ref
  40.8 2.0 copy.55
  42.8 2.0 copy.57
  45.1 1.9 slice.118.node_wb
  47.0 1.7 stack.23.feat_ref
  48.7 0.7 pad_bitcast_fusion.em_w1t
  49.4 1.9 maximum_bitcast_fusion.table_t
  51.2 2.0 broadcast_in_dim.17.vec
  53.2 1.3 broadcast_in_dim.16.em_vec
  54.6 77.9 %edge_fwd.1 = (bf16[512,8192]{1,0:T(8,128)(2,1)}, f32[512,8192]{1,0:T(8,128)}, f32[512,8192]{1,0:T(8,128)}, f32[1,8192]{1,0:T(1,128)}, f32[8,512,128]{2,1,0:T(8,128)}) custom-call(s32[32]{0:T(128)} %fusion.70.tile_ref, s32[8]{0:T(128)} %convert_element_type.82.fit_ref, s32[1]{0:T(128)} %bitcast.9.live_ref, f32[8,8192]{1,0:T(8,128)} %stack.23.feat_ref, ...), custom_call_target="tpu_custom_call" | custom-call | flops 38654705664 | bytes 67108864 | tf_op jit(solution)/shard_map/edge_fwd/pallas_call | solution.py:261
  132.5 2.7 convert_bitcast_fusion
  135.2 2.3 copy.59
  137.5 3.1 fusion
  140.6 0.9 add_reduce_fusion
  142.1 0.6 copy-done.8
  142.7 2.3 fusion.4
  145.1 2.7 multiply_convert_fusion
  147.7 1.7 copy.62
  149.5 1.5 pad_maximum_fusion.1.both_t
  151.0 46.7 %edge_bwd.1 = (f32[1536,512]{1,0:T(8,128)}, f32[512,512]{1,0:T(8,128)}, f32[768,512]{1,0:T(8,128)}) custom-call(s32[32]{0:T(128)} %fusion.70.tile_ref, s32[8]{0:T(128)} %convert_element_type.82.fit_ref, s32[1]{0:T(128)} %bitcast.9.live_ref, s32[1,8192]{1,0:T(1,128)} %bitcast.78, bf16[512,8192]{1,0:T(8,128)(2,1)} %get-tuple-element.24.he_ref, ...), custom_call_target="tpu_custom_call" | custom-call | flops 32212254720 | bytes 67108864 | tf_op jit(solution)/shard_map/edge_bwd/pallas_call | solution.py:285
  197.7 4.6 reshape.117
  202.7 5.0 pad_maximum_fusion
  207.6 1.0 copy-done.10
  210.6 3.1 copy.63
  213.7 1.8 fusion.79
  215.5 3.6 collective-permute-start.2
  219.2 1.9 collective-permute-start.3
  221.7 1.0 copy.66
  222.7 43.9 %collective-permute-done.3 = f32[128,512]{0,1:T(8,128)} collective-permute-done((f32[128,512]{0,1:T(8,128)S(1)}, f32[128,512]{0,1:T(8,128)}, u32[]{:S(2)}, u32[]{:S(2)}) %collective-permute-start.3) | collective-permute-done | bytes 262176 | tf_op jit(solution)/shard_map/ppermute | solution.py:308
  266.6 4.2 fusion.78
  270.8 3.5 fusion.13
  274.3 620.7 %reduce-scatter.2.cloned.1.call-done = f32[1,16,512]{2,1,0:T(8,128)} async-done(((f32[128,16,512]{2,1,0:T(8,128)}), f32[1,16,512]{2,1,0:T(8,128)}) %reduce-scatter.2.cloned.1.call-update) | async-done | bytes 32784 | tf_op jit(solution)/shard_map/reduce_scatter | solution.py:305
  895.0 1.4 slice_bitcast_fusion
  896.3 1.3 slice_bitcast_fusion.1
  (118 shorter events, 6.4 us)
Async XLA Ops:
  7.2 133.4 %copy-start = (bf16[512,512]{1,0:T(8,128)(2,1)S(1)}, bf16[512,512]{1,0:T(8,128)(2,1)}, u32[]{:S(2)}) copy-start(bf16[512,512]{1,0:T(8,128)(2,1)} %param.45) | copy-start | bytes 1572868
  7.2 887.8 %reduce-scatter.2.cloned.1.call-start = ((), (), s32[]{:S(2)}) async-start(), calls=%async_computation.1 | async-start | bytes 4227072 | tf_op jit(solution)/shard_map/reduce_scatter | solution.py:305
  8.1 3.9 copy-start.19
  8.1 3.9 copy-start.21
  9.7 2.0 copy-start.6
  11.7 1.0 copy-start.2
  11.7 8.4 copy-start.12
  11.7 8.5 copy-start.13
  11.8 9.2 %copy-start.14 = (s32[8192]{0:T(1024)S(1)}, s32[8192]{0:T(1024)}, u32[]{:S(2)}) copy-start(s32[8192]{0:T(1024)} %param.29) | copy-start | bytes 98308
  11.8 9.2 %copy-start.15 = (s32[8192]{0:T(1024)S(1)}, s32[8192]{0:T(1024)}, u32[]{:S(2)}) copy-start(s32[8192]{0:T(1024)} %param.30) | copy-start | bytes 98308
  11.8 16.4 %copy-start.31 = (f32[4,512]{1,0:T(4,128)S(1)}, f32[4,512]{1,0:T(4,128)}, u32[]{:S(2)}) copy-start(f32[4,512]{1,0:T(4,128)} %param.37) | copy-start | bytes 24580
  11.8 16.5 %copy-start.37 = (f32[1024,3]{0,1:T(4,128)S(1)}, f32[1024,3]{0,1:T(4,128)}, u32[]{:S(2)}) copy-start(f32[1024,3]{0,1:T(4,128)} %param.27) | copy-start | bytes 36868
  11.8 16.5 %copy-start.38 = (bf16[3,512]{1,0:T(4,128)(2,1)S(1)}, bf16[3,512]{1,0:T(4,128)(2,1)}, u32[]{:S(2)}) copy-start(bf16[3,512]{1,0:T(4,128)(2,1)} %param.35) | copy-start | bytes 9220
  12.0 8.1 copy-start.17
  13.6 35.7 %collective-permute-start = (bf16[128,512]{0,1:T(8,128)(2,1)}, bf16[128,512]{0,1:T(8,128)(2,1)S(1)}, u32[]{:S(2)}, u32[]{:S(2)}) collective-permute-start(bf16[128,512]{0,1:T(8,128)(2,1)} %get-tuple-element.60), channel_id=1, source_target_pairs={{0,1},{1,2},{2,3},{3,4},{4,5},{5,6},{6,7},{7,8},{8,9},{9,10},{10,1... | collective-permute-start | bytes 393224 | tf_op jit(solution)/shard_map/ppermute | solution.py:235
  18.1 31.2 %collective-permute-start.1 = (bf16[128,512]{0,1:T(8,128)(2,1)}, bf16[128,512]{0,1:T(8,128)(2,1)}, u32[]{:S(2)}, u32[]{:S(2)}) collective-permute-start(bf16[128,512]{0,1:T(8,128)(2,1)} %get-tuple-element.61), channel_id=1, source_target_pairs={{1,0},{2,1},{3,2},{4,3},{5,4},{6,5},{7,6},{8,7},{9,8},{10,9},{11,1... | collective-permute-start | bytes 393224 | tf_op jit(solution)/shard_map/ppermute | solution.py:234
  27.4 0.8 copy-start.16
  28.2 3.6 copy-start.24
  28.3 3.6 copy-start.26
  30.6 0.7 copy-start.32
  37.9 7.0 copy-start.34
  48.7 4.5 copy-start.28
  137.5 3.1 copy-start.23
  137.5 3.1 copy-start.35
  141.5 1.2 copy-start.8
  141.5 1.2 copy-start.25
  141.5 1.2 copy-start.27
  141.5 1.2 copy-start.29
  141.5 1.2 copy-start.30
  147.7 1.7 copy-start.4
  197.7 4.6 copy-start.7
  207.6 1.0 copy-start.10
  207.6 1.3 copy-start.33
  207.6 1.3 copy-start.9
  208.7 1.1 copy-start.36
  209.4 1.0 copy-start.5
  210.6 10.5 %copy-start.3 = (f32[512,512]{0,1:T(8,128)S(1)}, f32[512,512]{0,1:T(8,128)}, u32[]{:S(2)}) copy-start(f32[512,512]{0,1:T(8,128)} %copy-done.2) | copy-start | bytes 3145732
  210.6 10.5 %copy-start.18 = (f32[512]{0:T(512)S(1)}, f32[512]{0:T(512)}, u32[]{:S(2)}) copy-start(f32[512]{0:T(512)} %copy-done.17) | copy-start | bytes 6148
  210.6 10.5 %copy-start.20 = (f32[1,512]{1,0:T(1,128)S(1)}, f32[1,512]{1,0:T(1,128)}, u32[]{:S(2)}) copy-start(f32[1,512]{1,0:T(1,128)} %copy-done.19) | copy-start | bytes 6148
  210.6 10.5 %copy-start.22 = (f32[1,512]{1,0:T(1,128)S(1)}, f32[1,512]{1,0:T(1,128)}, u32[]{:S(2)}) copy-start(f32[1,512]{1,0:T(1,128)} %copy-done.21) | copy-start | bytes 6148
  215.5 7.2 collective-permute-start.2
  219.2 47.4 %collective-permute-start.3 = (f32[128,512]{0,1:T(8,128)S(1)}, f32[128,512]{0,1:T(8,128)}, u32[]{:S(2)}, u32[]{:S(2)}) collective-permute-start(f32[128,512]{0,1:T(8,128)S(1)} %get-tuple-element.58), channel_id=1, source_target_pairs={{1,0},{2,1},{3,2},{4,3},{5,4},{6,5},{7,6},{8,7},{9,8},{10,9},{11,1... | collective-permute-start | bytes 786440 | tf_op jit(solution)/shard_map/ppermute | solution.py:308
  266.6 4.2 copy-start.11
  270.8 626.9 %copy-start.1 = (bf16[512,512]{1,0:T(8,128)(2,1)S(1)}, bf16[512,512]{1,0:T(8,128)(2,1)}, u32[]{:S(2)}) copy-start(bf16[512,512]{1,0:T(8,128)(2,1)} %param.45) | copy-start | bytes 1572868
Sparse Core Ops, SparseCore 0:
  207.8 687.1 reduce-scatter.1

commit v2 on v1

--- a/solution.py
+++ b/solution.py
@@ -13,6 +13,7 @@
 STEP = 1024
 BF = jnp.bfloat16
 F32 = jnp.float32
+MESH = pl.DeviceIdType.MESH
 
 
 def mm(lhs, rhs):
@@ -173,6 +174,117 @@
         table_out[...] = mm_t(hi, w1b[...]) + mm_t(mid, w1b[...]) + mm_t(lo, w1b[...])
 
 
+STRIDE = {'z': 32, 'y': 8, 'x': 2}
+ORDERS = (('x', 'y', 'z'), ('y', 'z', 'x'), ('z', 'x', 'y'))
+DIM = 4
+
+
+def scatter_kernel(w1_ref, w2_ref, g1_out, g2_out, pair1, pair2, *scratch):
+    full = scratch[0:3]
+    recv = (scratch[3:6], scratch[6:9], scratch[9:12])
+    part = (scratch[12:15], scratch[15:18])
+    done1, done2, pair_send, pair_recv, hop_send, hop_recv = scratch[18:]
+    me = lax.axis_index('graph')
+    core = me % 2
+    coord = {name: (me // stride) % DIM for name, stride in STRIDE.items()}
+    partner = me + 1 - 2 * core
+
+    def peer(name, hop):
+        there = (coord[name] + hop) % DIM
+        return there, me + (there - coord[name]) * STRIDE[name]
+
+    barrier = pltpu.get_barrier_semaphore()
+    others = [partner] + [peer(name, hop)[1] for name in STRIDE for hop in range(1, DIM)]
+    for other in others:
+        pl.semaphore_signal(barrier, inc=1, device_id={'graph': other}, device_id_type=MESH)
+    pl.semaphore_wait(barrier, len(others))
+
+    half = w1_ref.shape[-1] // 2
+    mine = pl.multiple_of(core * half, half)
+    theirs = pl.multiple_of((1 - core) * half, half)
+
+    def to_partner(src, dst, slot):
+        copy = pltpu.make_async_remote_copy(src_ref=src, dst_ref=dst, send_sem=pair_send.at[slot], recv_sem=pair_recv.at[slot],
+                                            device_id={'graph': partner}, device_id_type=MESH)
+        copy.start()
+        return copy
+
+    first = [to_partner(w1_ref.at[:, :, :, :, pl.ds(theirs, half)], pair1, 0),
+             to_partner(w2_ref.at[:, :, :, :, pl.ds(theirs, half)], pair2, 1)]
+    first[0].wait()
+    quarter = half // 2
+    full[0][...] = w1_ref[:, :, :, :, pl.ds(mine, quarter)] + pair1[:, :, :, :, :quarter]
+    full[1][...] = w1_ref[:, :, :, :, pl.ds(mine + quarter, quarter)] + pair1[:, :, :, :, quarter:]
+    first[1].wait()
+    full[2][...] = w2_ref[:, :, :, :, pl.ds(mine, half)] + pair2[...]
+
+    left = [list(STRIDE) for _ in range(3)]
+    held = list(full)
+
+    def at(color, name, index):
+        pos = left[color].index(name)
+        return (slice(None),) * pos + (index,)
+
+    for stage in range(3):
+        copies = []
+        for color in range(3):
+            name = ORDERS[color][stage]
+            for hop in range(1, DIM):
+                there, device = peer(name, hop)
+                copy = pltpu.make_async_remote_copy(
+                    src_ref=held[color].at[at(color, name, there)], dst_ref=recv[stage][color].at[hop - 1],
+                    send_sem=hop_send.at[stage, color, hop - 1], recv_sem=hop_recv.at[stage, color, hop - 1],
+                    device_id={'graph': device}, device_id_type=MESH)
+                copy.start()
+                copies.append(copy)
+        for color in range(3):
+            for copy in copies[3 * color:3 * color + 3]:
+                copy.wait()
+            name = ORDERS[color][stage]
+            got = recv[stage][color]
+            total = held[color][at(color, name, coord[name])] + got[0] + got[1] + got[2]
+            left[color].remove(name)
+            if stage < 2:
+                part[stage][color][...] = total
+                held[color] = part[stage][color]
+            elif color == 2:
+                done2[core] = total
+            else:
+                done1[core, :, color * quarter:(color + 1) * quarter] = total
+
+    last = [to_partner(done1.at[core], done1.at[core], 2), to_partner(done2.at[core], done2.at[core], 3)]
+    for copy in last:
+        copy.wait()
+    for done, out in ((done1, g1_out), (done2, g2_out)):
+        rows = out.shape[0]
+        whole = jnp.concatenate([done[0], done[1]], axis=1)
+        out[...] = jnp.where(core == 0, whole[:rows], whole[rows:])
+
+
+def scatter_call(w1, w2):
+    rows1, rows2, cols = w1.shape[-2], w2.shape[-2], w1.shape[-1]
+    half, quarter = cols // 2, cols // 4
+    tail = ((rows1, quarter), (rows1, quarter), (rows2, half))
+    scratch = [pltpu.VMEM((DIM,) * 3 + (rows1, half), F32), pltpu.VMEM((DIM,) * 3 + (rows2, half), F32)]
+    scratch += [pltpu.VMEM((DIM,) * 3 + t, F32) for t in tail]
+    for stage in range(3):
+        scratch += [pltpu.VMEM((3,) + (DIM,) * (2 - stage) + t, F32) for t in tail]
+    for stage in range(2):
+        scratch += [pltpu.VMEM((DIM,) * (2 - stage) + t, F32) for t in tail]
+    scratch += [pltpu.VMEM((2, rows1, half), F32), pltpu.VMEM((2, rows2, half), F32),
+                pltpu.SemaphoreType.DMA((4,)), pltpu.SemaphoreType.DMA((4,)),
+                pltpu.SemaphoreType.DMA((3, 3, 3)), pltpu.SemaphoreType.DMA((3, 3, 3))]
+    vm = pl.BlockSpec(memory_space=pltpu.VMEM)
+    return pl.pallas_call(
+        scatter_kernel,
+        in_specs=[vm, vm], out_specs=[vm, vm],
+        out_shape=[jax.ShapeDtypeStruct((rows1 // 2, cols), F32), jax.ShapeDtypeStruct((rows2 // 2, cols), F32)],
+        scratch_shapes=scratch,
+        compiler_params=pltpu.CompilerParams(collective_id=0, has_side_effects=True, vmem_limit_bytes=40 * 2 ** 20),
+        name="weight_scatter",
+    )(w1, w2)
+
+
 def mlp_forward(x_in, w_one, w_two, vec_rows):
     pre_one = jnp.dot(x_in, w_one, preferred_element_type=jnp.float32) + vec_rows[0]
     act_bf = jax.nn.silu(pre_one).astype(jnp.bfloat16)
@@ -301,9 +413,8 @@
             name="edge_bwd",
         )(first_tile, fits, live, *bwd_in)
 
-        w_parts = jnp.concatenate([w1_part.reshape(groups, -1, latent), w2_part.reshape(groups, -1, latent)], axis=1)
-        w_sum = lax.psum_scatter(w_parts, 'graph', scatter_dimension=0, tiled=True)[0]
-        w1_grad, w2_grad = w_sum[:w1_part.shape[0] // groups], w_sum[w1_part.shape[0] // groups:]
+        chips = (DIM, DIM, DIM)
+        w1_grad, w2_grad = scatter_call(w1_part.reshape(chips + (-1, latent)), w2_part.reshape(chips + (-1, latent)))
 
         tail_grad = lax.ppermute(table_grad[:halo_rows], 'graph', down_perm)
         head_grad = lax.ppermute(table_grad[band_rows + halo_rows:], 'graph', up_perm)

time: 913 us -> 300 us (0.33)
  waiting for transfers between devices: 665 us -> 0.01 us
  Pallas kernels: 125 us -> 188 us
  between operations: 14.9 us -> 1.55 us
  starting transfers between devices: 12 us -> 24.5 us
    reduce_scatter x1 -> x0, waiting for transfers between devices: 621 us -> none  [device_step(): lax.psum_scatter(w_parts, 'graph', scatter_dimension=0, tiled=True)[0]]
    pallas_call x0 -> x1, Pallas kernels: none -> 50 us  [scatter_call(): pl.pallas_call(scatter_kernel, in_specs=[vm, vm], out_specs=[vm, vm], out...]
    ppermute x1, waiting for transfers between devices: 43.9 us -> 0.01 us  [device_step(): tail_grad = lax.ppermute(table_grad[:halo_rows], 'graph', down_perm)]
    ppermute x1, starting transfers between devices: 3.63 us -> 16.2 us  [device_step(): lax.ppermute(table_grad[band_rows + halo_rows:], 'graph', up_perm)]
  transfers between devices with their start and end apart: 5 -> 4, of which waited for: 2 -> 0; matrix products, arithmetic and copies ran while one was open for 5% -> 14% of each run, Pallas kernels for 0% -> 17%
where the time goes in v2:
time: 300 us; the launch traced here: 298 us
  Pallas kernels  188 us (63%)
  local copies, waits for them, and re-layouts  35.9 us (12%)
  other arithmetic  25 us (8%)
  starting transfers between devices  24.5 us (8%)
  matrix products  23.1 us (8%)
    pallas_call x1, Pallas kernels, device_step(): pl.pallas_call(functools.partial(edge_fwd_kernel, mesh_tiles, table_rows)...  86.7 us
    pallas_call x1, Pallas kernels, device_step(): pl.pallas_call(functools.partial(edge_bwd_kernel, mesh_tiles, table_rows,...  51.2 us
    pallas_call x1, Pallas kernels, scatter_call(): pl.pallas_call(scatter_kernel, in_specs=[vm, vm], out_specs=[vm, vm], out...  50 us
    ppermute x1, starting transfers between devices, device_step(): lax.ppermute(table_grad[band_rows + halo_rows:], 'graph', up_perm)  16.2 us
    unnamed x94, local copies, waits for them, and re-layouts  15.5 us
    dot_general x4, matrix products, mlp_forward(): jnp.dot(act_bf, w_two, preferred_element_type=jnp.float32) + vec_rows[1]  6.74 us
    sort x1, other arithmetic, device_step(): lax.sort((key, feat_t[0], feat_t[1], feat_t[2], feat_t[3]), num_keys=1, i...  6.49 us
    dot_general x3, matrix products, mlp_forward(): jnp.dot(x_in, w_one, preferred_element_type=jnp.float32) + vec_rows[0]  6.19 us
  transfers between devices with their start and end apart: 4, of which 0 were waited for; matrix products, arithmetic and copies ran while one was open for 14% of the time, Pallas kernels for 17%

profile of v2, /device:TPU:1, one launch (start us, length us, event | category | flops | bytes accessed | tf_op | source)
XLA Modules:
  0.0 298.2 jit_solution(546592184197581647)
XLA Ops:
  0.6 0.9 fusion.84
  1.5 1.6 convolution_add_fusion.4
  3.1 2.0 fusion.86
  5.4 0.7 copy-done.4
  6.4 0.7 fusion.80
  7.1 4.5 %collective-permute-start = (bf16[128,512]{0,1:T(8,128)(2,1)}, bf16[128,512]{0,1:T(8,128)(2,1)S(1)}, u32[]{:S(2)}, u32[]{:S(2)}) collective-permute-start(bf16[128,512]{0,1:T(8,128)(2,1)} %get-tuple-element.64), channel_id=1, source_target_pairs={{0,1},{1,2},{2,3},{3,4},{4,5},{5,6},{6,7},{7,8},{8,9},{9,10},{10,1... | collective-permute-start | bytes 393224 | tf_op jit(solution)/shard_map/ppermute | solution.py:347
  11.6 1.9 collective-permute-start.1
  13.7 0.6 convert_reduce_fusion
  14.3 6.5 %sort.33 = (s32[8192]{0:T(1024)S(1)}, f32[8192]{0:T(1024)}, f32[8192]{0:T(1024)}, f32[8192]{0:T(1024)}, f32[8192]{0:T(1024)}) sort(s32[8192]{0:T(1024)S(1)} %add_select_fusion, f32[8192]{0:T(1024)S(1)} %bitcast.72, f32[8192]{0:T(1024)S(1)} %bitcast.71, f32[8192]{0:T(1024)S(1)} %bitcast.70, f32[8192]{0:T(1024)S(1)} %bitcast.69), dimensions={0}, to_apply=%region_2.3 | sort | flops 106496 | bytes 327680 | tf_op jit(solution)/shard_map/sort | solution.py:353
  21.6 2.3 add_reduce_fusion.1
  25.9 1.5 convolution_add_fusion.2
  27.4 1.6 fusion.89
  29.0 1.4 multiply_reduce_fusion.4
  30.9 1.5 add_convert_fusion.1
  32.5 2.6 copy.56
  35.1 1.9 slice.107.w1b
  37.0 2.3 copy.58
  39.8 2.0 copy.55
  41.8 2.0 copy.57
  44.1 1.9 slice.106.node_wb
  46.0 2.0 copy.61
  48.0 1.7 stack.23.feat_ref
  49.8 0.7 pad_bitcast_fusion.em_w1t
  50.4 1.9 maximum_bitcast_fusion.table_t
  52.3 2.0 broadcast_in_dim.17.vec
  54.3 1.3 broadcast_in_dim.16.em_vec
  55.6 86.7 %edge_fwd.1 = (bf16[512,8192]{1,0:T(8,128)(2,1)}, f32[512,8192]{1,0:T(8,128)}, f32[512,8192]{1,0:T(8,128)}, f32[1,8192]{1,0:T(1,128)}, f32[8,512,128]{2,1,0:T(8,128)}) custom-call(s32[32]{0:T(128)} %fusion.70.tile_ref, s32[8]{0:T(128)} %convert_element_type.82.fit_ref, s32[1]{0:T(128)} %bitcast.9.live_ref, f32[8,8192]{1,0:T(8,128)} %stack.23.feat_ref, ...), custom_call_target="tpu_custom_call" | custom-call | flops 38654705664 | bytes 67108864 | tf_op jit(solution)/shard_map/edge_fwd/pallas_call | solution.py:373
  142.4 2.7 convert_bitcast_fusion
  145.1 2.3 copy.59
  147.4 3.1 %fusion = f32[1024,512]{1,0:T(8,128)S(1)} fusion(bf16[1024,512]{1,0:T(8,128)(2,1)} %param.44, bf16[1024,512]{1,0:T(8,128)(2,1)} %bitcast.65, bf16[1024,512]{1,0:T(8,128)(2,1)} %add_convert_fusion.1), kind=kOutput, calls=%fused_computation | convolution fusion | flops 1077936128 | bytes 5242880 | tf_op jit(solution)/shard_map/dot_general | solution.py:289
  150.5 0.9 add_reduce_fusion
  152.0 0.6 copy-done.11
  152.6 2.3 fusion.4
  155.0 1.9 multiply_convert_fusion
  156.9 0.7 copy.62
  158.1 1.5 pad_maximum_fusion.both_t
  159.6 51.2 %edge_bwd.1 = (f32[1536,512]{1,0:T(8,128)}, f32[512,512]{1,0:T(8,128)}, f32[768,512]{1,0:T(8,128)}) custom-call(s32[32]{0:T(128)} %fusion.70.tile_ref, s32[8]{0:T(128)} %convert_element_type.82.fit_ref, s32[1]{0:T(128)} %bitcast.9.live_ref, s32[1,8192]{1,0:T(1,128)} %bitcast.78, bf16[512,8192]{1,0:T(8,128)(2,1)} %get-tuple-element.26.he_ref, ...), custom_call_target="tpu_custom_call" | custom-call | flops 32212254720 | bytes 67108864 | tf_op jit(solution)/shard_map/edge_bwd/pallas_call | solution.py:397
  210.8 1.9 copy.63
  212.7 0.8 fusion.79
  213.5 16.2 %collective-permute-start.2 = (f32[128,512]{0,1:T(8,128)}, f32[128,512]{0,1:T(8,128)}, u32[]{:S(2)}, u32[]{:S(2)}) collective-permute-start(f32[128,512]{0,1:T(8,128)} %get-tuple-element.61), channel_id=1, source_target_pairs={{0,1},{1,2},{2,3},{3,4},{4,5},{5,6},{6,7},{7,8},{8,9},{9,10},{10,1... | collective-permute-start | bytes 786440 | tf_op jit(solution)/shard_map/ppermute | solution.py:420
  229.7 1.9 collective-permute-start.3
  231.8 3.2 %fusion.10 = (f32[512]{0:T(512)S(1)}, f32[512]{0:T(512)S(1)}, bf16[512,512]{0,1:T(8,128)(2,1)}) fusion(bf16[512,512]{0,1:T(8,128)(2,1)} %copy.61, f32[512]{0:T(512)S(1)} %bitcast.96, f32[512]{0:T(512)S(1)} %copy-done.32, f32[512,512]{0,1:T(8,128)} %get-tuple-element.93, f32[512]{0:T(512)S(1)} %copy-done.21, f32[512]{0:T(512)S(1)} %bitcast.98, ...), kind=kLoop, calls=%fused_computation.33 | loop fusion | flops 4455424 | bytes 3166208 | tf_op jit(solution)/shard_map/reduce_sum | solution.py:301
  235.0 2.0 copy.66
  237.0 1.2 copy-done.3
  238.3 50.0 %weight_scatter.1 = (f32[12,512]{1,0:T(8,128)S(1)}, f32[4,512]{1,0:T(4,128)S(1)}) custom-call(f32[4,4,4,24,512]{4,3,2,1,0:T(8,128)S(1)} %bitcast.57, f32[4,4,4,8,512]{4,3,2,1,0:T(8,128)S(1)} %bitcast.58), custom_call_target="tpu_custom_call" | custom-call | tf_op jit(solution)/shard_map/weight_scatter/pallas_call | solution.py:278
  288.3 5.2 %fusion.78 = (f32[512]{0:T(512)S(1)}, f32[512]{0:T(512)S(1)}, f32[512,512]{0,1:T(8,128)}) fusion(f32[512]{0:T(512)S(1)} %copy-done.19, f32[512,512]{0,1:T(8,128)} %copy-done.4, f32[512]{0:T(512)S(1)} %broadcast_multiply_fusion.9, f32[512]{0:T(512)S(1)} %bitcast.85, f32[128,512]{0,1:T(8,128)} %collective-permute-done.3, f32[512]{0:T(512)S(1)} %pad.6.clone, ...), kind=kOutput, calls=%fused_computation.133 | convolution fusion | flops 544734208 | bytes 7886848 | tf_op jit(solution)/shard_map/nj,kj->nk/dot_general | solution.py:424
  293.6 3.1 %fusion.13 = f32[512,267]{0,1:T(8,128)} fusion(bf16[267,512]{1,0:T(8,128)(2,1)S(1)} %copy-done.12, bf16[512,512]{1,0:T(8,128)(2,1)} %param.33, f32[512,512]{1,0:T(8,128)S(1)} %copy-done.10, f32[512,512]{0,1:T(8,128)} %get-tuple-element.94, f32[512,512]{0,1:T(8,128)S(1)} %copy-done.5, f32[512]{0:T(512)S(1)} %broadcast_multiply_fusion.4, ...), kind=kOutput, calls=%fused_computation.36 | convolution fusion | flops 412614656 | bytes 4498432 | tf_op jit(solution)/shard_map/nj,kj->nk/dot_general | solution.py:428
  296.7 0.6 copy.70
  (121 shorter events, 6.5 us)
Async XLA Ops:
  0.6 149.9 %copy-start = (bf16[512,512]{1,0:T(8,128)(2,1)S(1)}, bf16[512,512]{1,0:T(8,128)(2,1)}, u32[]{:S(2)}) copy-start(bf16[512,512]{1,0:T(8,128)(2,1)} %param.45) | copy-start | bytes 1572868
  1.5 3.9 %copy-start.22 = (f32[1,512]{1,0:T(1,128)}, f32[1,512]{1,0:T(1,128)S(1)}, u32[]{:S(2)}) copy-start(f32[1,512]{1,0:T(1,128)S(1)} %get-tuple-element.78) | copy-start | bytes 6148
  1.5 3.9 %copy-start.24 = (f32[1,512]{1,0:T(1,128)}, f32[1,512]{1,0:T(1,128)S(1)}, u32[]{:S(2)}) copy-start(f32[1,512]{1,0:T(1,128)S(1)} %get-tuple-element.81) | copy-start | bytes 6148
  3.1 2.0 copy-start.9
  5.1 1.0 copy-start.4
  5.2 8.4 %copy-start.13 = (f32[8192,4]{0,1:T(4,128)S(1)}, f32[8192,4]{0,1:T(4,128)}, u32[]{:S(2)}) copy-start(f32[8192,4]{0,1:T(4,128)} %param.28) | copy-start | bytes 393220
  5.2 8.5 %copy-start.14 = (s32[8192]{0:T(1024)S(1)}, s32[8192]{0:T(1024)}, u32[]{:S(2)}) copy-start(s32[8192]{0:T(1024)} %param.31) | copy-start | bytes 98308
  5.2 9.1 %copy-start.15 = (s32[8192]{0:T(1024)S(1)}, s32[8192]{0:T(1024)}, u32[]{:S(2)}) copy-start(s32[8192]{0:T(1024)} %param.29) | copy-start | bytes 98308
  5.2 9.1 %copy-start.16 = (s32[8192]{0:T(1024)S(1)}, s32[8192]{0:T(1024)}, u32[]{:S(2)}) copy-start(s32[8192]{0:T(1024)} %param.30) | copy-start | bytes 98308
  5.2 16.4 %copy-start.37 = (f32[4,512]{1,0:T(4,128)S(1)}, f32[4,512]{1,0:T(4,128)}, u32[]{:S(2)}) copy-start(f32[4,512]{1,0:T(4,128)} %param.37) | copy-start | bytes 24580
  5.4 8.1 %copy-start.18 = (f32[512]{0:T(512)}, f32[512]{0:T(512)S(1)}, u32[]{:S(2)}) copy-start(f32[512]{0:T(512)S(1)} %add_rsqrt_fusion.3) | copy-start | bytes 6148
  7.1 43.4 %collective-permute-start = (bf16[128,512]{0,1:T(8,128)(2,1)}, bf16[128,512]{0,1:T(8,128)(2,1)S(1)}, u32[]{:S(2)}, u32[]{:S(2)}) collective-permute-start(bf16[128,512]{0,1:T(8,128)(2,1)} %get-tuple-element.64), channel_id=1, source_target_pairs={{0,1},{1,2},{2,3},{3,4},{4,5},{5,6},{6,7},{7,8},{8,9},{9,10},{10,1... | collective-permute-start | bytes 393224 | tf_op jit(solution)/shard_map/ppermute | solution.py:347
  11.6 38.9 %collective-permute-start.1 = (bf16[128,512]{0,1:T(8,128)(2,1)}, bf16[128,512]{0,1:T(8,128)(2,1)}, u32[]{:S(2)}, u32[]{:S(2)}) collective-permute-start(bf16[128,512]{0,1:T(8,128)(2,1)} %get-tuple-element.65), channel_id=1, source_target_pairs={{1,0},{2,1},{3,2},{4,3},{5,4},{6,5},{7,6},{8,7},{9,8},{10,9},{11,1... | collective-permute-start | bytes 393224 | tf_op jit(solution)/shard_map/ppermute | solution.py:346
  20.8 3.2 %copy-start.17 = (s32[8192]{0:T(1024)}, s32[8192]{0:T(1024)S(1)}, u32[]{:S(2)}) copy-start(s32[8192]{0:T(1024)S(1)} %get-tuple-element.20) | copy-start | bytes 98308
  21.6 9.3 %copy-start.27 = (f32[1,512]{1,0:T(1,128)}, f32[1,512]{1,0:T(1,128)S(1)}, u32[]{:S(2)}) copy-start(f32[1,512]{1,0:T(1,128)S(1)} %get-tuple-element.84) | copy-start | bytes 6148
  21.6 9.3 %copy-start.29 = (f32[1,512]{1,0:T(1,128)}, f32[1,512]{1,0:T(1,128)S(1)}, u32[]{:S(2)}) copy-start(f32[1,512]{1,0:T(1,128)S(1)} %get-tuple-element.85) | copy-start | bytes 6148
  24.0 0.7 copy-start.38
  24.0 1.3 copy-start.39
  24.7 2.7 copy-start.42
  27.4 1.6 copy-start.8
  29.0 3.4 %copy-start.20 = (f32[512]{0:T(512)}, f32[512]{0:T(512)S(1)}, u32[]{:S(2)}) copy-start(f32[512]{0:T(512)S(1)} %broadcast_multiply_fusion.8) | copy-start | bytes 6148
  37.0 6.9 %copy-start.40 = (bf16[4,512]{1,0:T(4,128)(2,1)S(1)}, bf16[4,512]{1,0:T(4,128)(2,1)}, u32[]{:S(2)}) copy-start(bf16[4,512]{1,0:T(4,128)(2,1)} %param.38) | copy-start | bytes 12292
  49.8 4.6 %copy-start.31 = (f32[4,512]{1,0:T(4,128)S(1)}, f32[4,512]{1,0:T(4,128)}, u32[]{:S(2)}) copy-start(f32[4,512]{1,0:T(4,128)} %param.40) | copy-start | bytes 24580
  147.4 3.1 %copy-start.26 = (f32[1,512]{1,0:T(1,128)S(1)}, f32[1,512]{1,0:T(1,128)}, u32[]{:S(2)}) copy-start(f32[1,512]{1,0:T(1,128)} %get-tuple-element.74) | copy-start | bytes 6148
  147.4 3.1 %copy-start.41 = (f32[1,512]{1,0:T(1,128)S(1)}, f32[1,512]{1,0:T(1,128)}, u32[]{:S(2)}) copy-start(f32[1,512]{1,0:T(1,128)} %get-tuple-element.75) | copy-start | bytes 6148
  151.4 1.2 copy-start.11
  151.4 1.2 copy-start.28
  151.4 1.2 copy-start.30
  151.4 1.2 copy-start.35
  151.4 1.2 copy-start.36
  156.8 1.2 copy-start.6
  210.8 20.9 %copy-start.19 = (f32[512]{0:T(512)S(1)}, f32[512]{0:T(512)}, u32[]{:S(2)}) copy-start(f32[512]{0:T(512)} %copy-done.18) | copy-start | bytes 6148
  210.8 20.9 %copy-start.21 = (f32[512]{0:T(512)S(1)}, f32[512]{0:T(512)}, u32[]{:S(2)}) copy-start(f32[512]{0:T(512)} %copy-done.20) | copy-start | bytes 6148
  210.8 20.9 %copy-start.23 = (f32[1,512]{1,0:T(1,128)S(1)}, f32[1,512]{1,0:T(1,128)}, u32[]{:S(2)}) copy-start(f32[1,512]{1,0:T(1,128)} %copy-done.22) | copy-start | bytes 6148
  210.8 20.9 %copy-start.25 = (f32[1,512]{1,0:T(1,128)S(1)}, f32[1,512]{1,0:T(1,128)}, u32[]{:S(2)}) copy-start(f32[1,512]{1,0:T(1,128)} %copy-done.24) | copy-start | bytes 6148
  210.8 20.9 %copy-start.32 = (f32[512]{0:T(512)S(1)}, f32[512]{0:T(512)}, u32[]{:S(2)}) copy-start(f32[512]{0:T(512)} %add_rsqrt_fusion.2) | copy-start | bytes 6148
  210.8 20.9 %copy-start.33 = (f32[1,512]{1,0:T(1,128)S(1)}, f32[1,512]{1,0:T(1,128)}, u32[]{:S(2)}) copy-start(f32[1,512]{1,0:T(1,128)} %get-tuple-element.70) | copy-start | bytes 6148
  210.8 20.9 %copy-start.34 = (f32[1,512]{1,0:T(1,128)S(1)}, f32[1,512]{1,0:T(1,128)}, u32[]{:S(2)}) copy-start(f32[1,512]{1,0:T(1,128)} %get-tuple-element.73) | copy-start | bytes 6148
  212.7 19.0 %copy-start.7 = (f32[768,512]{0,1:T(8,128)}, f32[768,512]{0,1:T(8,128)S(1)}, u32[]{:S(2)}) copy-start(f32[768,512]{0,1:T(8,128)S(1)} %copy.63) | copy-start | bytes 4718596
  213.5 74.8 %collective-permute-start.2 = (f32[128,512]{0,1:T(8,128)}, f32[128,512]{0,1:T(8,128)}, u32[]{:S(2)}, u32[]{:S(2)}) collective-permute-start(f32[128,512]{0,1:T(8,128)} %get-tuple-element.61), channel_id=1, source_target_pairs={{0,1},{1,2},{2,3},{3,4},{4,5},{5,6},{6,7},{7,8},{8,9},{9,10},{10,1... | collective-permute-start | bytes 786440 | tf_op jit(solution)/shard_map/ppermute | solution.py:420
  229.7 58.6 %collective-permute-start.3 = (f32[128,512]{0,1:T(8,128)S(1)}, f32[128,512]{0,1:T(8,128)}, u32[]{:S(2)}, u32[]{:S(2)}) collective-permute-start(f32[128,512]{0,1:T(8,128)S(1)} %get-tuple-element.62), channel_id=1, source_target_pairs={{1,0},{2,1},{3,2},{4,3},{5,4},{6,5},{7,6},{8,7},{9,8},{10,9},{11,1... | collective-permute-start | bytes 786440 | tf_op jit(solution)/shard_map/ppermute | solution.py:419
  231.7 5.3 %copy-start.2 = (f32[1536,512]{1,0:T(8,128)S(1)}, f32[1536,512]{1,0:T(8,128)}, u32[]{:S(2)}) copy-start(f32[1536,512]{1,0:T(8,128)} %get-tuple-element.31) | copy-start | bytes 9437188
  237.0 1.2 copy-start.3
  288.3 5.3 %copy-start.5 = (f32[512,512]{0,1:T(8,128)S(1)}, f32[512,512]{0,1:T(8,128)}, u32[]{:S(2)}) copy-start(f32[512,512]{0,1:T(8,128)} %copy-done.4) | copy-start | bytes 3145732
  288.3 5.3 %copy-start.10 = (f32[512,512]{1,0:T(8,128)S(1)}, f32[512,512]{1,0:T(8,128)}, u32[]{:S(2)}) copy-start(f32[512,512]{1,0:T(8,128)} %copy-done.9) | copy-start | bytes 3145732
  288.3 5.3 %copy-start.12 = (bf16[267,512]{1,0:T(8,128)(2,1)S(1)}, bf16[267,512]{1,0:T(8,128)(2,1)}, u32[]{:S(2)}) copy-start(bf16[267,512]{1,0:T(8,128)(2,1)} %param.32) | copy-start | bytes 820228
  293.6 4.3 %copy-start.1 = (bf16[512,512]{1,0:T(8,128)(2,1)S(1)}, bf16[512,512]{1,0:T(8,128)(2,1)}, u32[]{:S(2)}) copy-start(bf16[512,512]{1,0:T(8,128)(2,1)} %param.45) | copy-start | bytes 1572868

commit v3 on v2

v3 whole, which is shorter than its diff:
```python
import jax
import jax.numpy as jnp
from jax import lax
from jax.experimental import pallas as pl
from jax.experimental.pallas import tpu as pltpu
from jax.sharding import PartitionSpec as P

NORM_EPS = 1e-5
LANES = 128
SUB = 512
STEP = 1024
KEY_BITS = 10
BF = jnp.bfloat16
F32 = jnp.float32
MESH = pl.DeviceIdType.MESH


def mm(lhs, rhs):
    return jnp.dot(lhs, rhs, preferred_element_type=F32)


def mm_t(lhs, rhs):
    return lax.dot_general(lhs, rhs, (((1,), (1,)), ((), ())), preferred_element_type=F32)


def split3(val):
    hi = val.astype(BF)
    rest = val - hi.astype(F32)
    mid = rest.astype(BF)
    lo = (rest - mid.astype(F32)).astype(BF)
    return hi, mid, lo


def sigmoid(val):
    return 0.5 * jnp.tanh(0.5 * val) + 0.5


def lanes_of(col, width):
    return jnp.concatenate([col] * (width // LANES), axis=1)


def one_hot(ids_row, first, rows):
    row_ids = lax.broadcasted_iota(jnp.int32, (rows, ids_row.shape[1]), 0) + first
    return jnp.where(row_ids == ids_row, 1.0, 0.0).astype(BF)


def norm_fwd(val):
    mean = jnp.mean(val, axis=0, keepdims=True)
    centred = val - mean
    inv = lax.rsqrt(jnp.mean(centred * centred, axis=0, keepdims=True) + NORM_EPS)
    return centred * inv, mean, inv


def norm_bwd(d_norm, normed, inv):
    return inv * (d_norm - jnp.mean(d_norm, axis=0, keepdims=True)
                  - normed * jnp.mean(d_norm * normed, axis=0, keepdims=True))


def edge_kernel(first_ref, fit_ref, live_ref, feat_ref, key_ref, mesh_x, below, band, above, small_w, em_w2, mesh_w2,
                w1, w2, node_w1, node_w2, vecs, cot_ref, mesh_out, w1_out, w2_out, table_out,
                em_w2t, w1t, w2t, table_t, both_t, vec_b, pre_buf, he_buf, mean_buf, inv_buf, agg_buf,
                g1_buf, g2_buf, act_buf, hm_buf, hot_buf):
    latent = w2.shape[0]
    table_rows = table_t.shape[1]
    mesh_tiles = both_t.shape[0]
    per_sub = SUB // LANES
    eye = one_hot(lax.broadcasted_iota(jnp.int32, (1, latent), 1), 0, latent)
    turned = lambda val: mm_t(eye, val).astype(BF)

    em_w2t[...] = turned(em_w2[...])
    w2t[...] = turned(w2[...])
    for part in range(3):
        w1t[:, part * latent:(part + 1) * latent] = turned(w1[part * latent:(part + 1) * latent])
    at = 0
    for piece in (below, band, above):
        rows = piece.shape[0]
        table_t[:, at:at + rows] = turned(piece[...])
        at += rows
    cols = jnp.transpose(vecs[...])
    col = lambda mlp, row: cols[:, 4 * mlp + row:4 * mlp + row + 1]
    for row in range(4):
        vec_b[row] = jnp.broadcast_to(col(0, row), (latent, LANES))
        vec_b[4 + row] = jnp.broadcast_to(col(2, row), (latent, LANES))
    small_t = turned(small_w[...])
    agg_buf[...] = jnp.zeros_like(agg_buf)
    w1_out[...] = jnp.zeros_like(w1_out)
    w2_out[...] = jnp.zeros_like(w2_out)
    table_out[...] = jnp.zeros_like(table_out)

    mesh_w2t = turned(mesh_w2[...])
    for blk in range(mesh_tiles // per_sub):
        pre = mm(small_t[:, 8:], mesh_x[:, blk * SUB:(blk + 1) * SUB].astype(BF)) + col(1, 0)
        act = (pre * sigmoid(pre)).astype(BF)
        normed, _, _ = norm_fwd(mm(mesh_w2t, act) + col(1, 1))
        hm = (normed * col(1, 2) + col(1, 3)).astype(BF)
        for idx in range(per_sub):
            both_t[blk * per_sub + idx, :latent] = hm[:, idx * LANES:(idx + 1) * LANES]

    vec_at = lambda row: lanes_of(vec_b[row], SUB)

    def edges_of(sub, whole):
        span = pl.ds(pl.multiple_of(sub * SUB, SUB), SUB)
        key = key_ref[:, span]
        dst = key >> KEY_BITS
        if whole:
            tiles = list(range(mesh_tiles))
            hot = one_hot(dst, 0, mesh_tiles * LANES)
        else:
            first = first_ref[sub]
            tiles = [first, first + 1]
            hot = one_hot(dst, first * LANES, 2 * LANES)
        return span, one_hot(key & (2 ** KEY_BITS - 1), 0, table_rows), tiles, hot

    def forward(sub, whole):
        span, src_hot, tiles, hot = edges_of(sub, whole)
        pre = mm(small_t[:, :8], feat_ref[:, span].astype(BF)) + vec_at(0)
        act = (pre * sigmoid(pre)).astype(BF)
        normed, _, _ = norm_fwd(mm(em_w2t[...], act) + vec_at(1))
        he = (normed * vec_at(2) + vec_at(3)).astype(BF)
        he_buf[:, span] = he
        hg = mm(table_t[...], src_hot).astype(BF)
        hm = mm(jnp.concatenate([both_t[t, :latent] for t in tiles], axis=1), hot).astype(BF)
        pre = mm(w1t[:, :latent], he) + mm(w1t[:, latent:2 * latent], hg) + mm(w1t[:, 2 * latent:], hm) + vec_at(4)
        pre_buf[:, span] = pre
        act = (pre * sigmoid(pre)).astype(BF)
        normed, mean, inv = norm_fwd(mm(w2t[...], act) + vec_at(5))
        mean_buf[:, span] = mean
        inv_buf[:, span] = inv
        hi, mid, lo = split3(he.astype(F32) + (normed * vec_at(6) + vec_at(7)))
        add = mm_t(hi, hot) + mm_t(mid, hot) + mm_t(lo, hot)
        for idx, tile in enumerate(tiles):
            agg_buf[tile] += add[:, idx * LANES:(idx + 1) * LANES]

    def backward(sub, whole, slot):
        span, src_hot, tiles, hot = edges_of(sub, whole)
        to = pl.ds(pl.multiple_of(slot * SUB, SUB), SUB)
        both = mm(jnp.concatenate([both_t[t] for t in tiles], axis=1), hot).astype(BF)
        hm_buf[:, to] = both[:latent]
        hot_buf[:, to] = src_hot
        pre = pre_buf[:, span]
        sig = sigmoid(pre)
        act = (pre * sig).astype(BF)
        act_buf[:, to] = act
        inv = inv_buf[:, span]
        normed = (mm(w2t[...], act) + vec_at(5) - mean_buf[:, span]) * inv
        d_norm = mm(node_w1[latent:], both[latent:]) * vec_at(6)
        g_two = norm_bwd(d_norm, normed, inv).astype(BF)
        g2_buf[:, to] = g_two
        g1_buf[:, to] = (mm(w2[...], g_two) * sig * (1.0 + pre * (1.0 - sig))).astype(BF)

    pairs = (live_ref[0] + STEP - 1) // STEP
    per_step = STEP // SUB

    @pl.loop(0, pairs)
    def _(step):
        fit = fit_ref[step] == 1

        @pl.when(fit)
        def _():
            for sub in range(per_step):
                forward(step * per_step + sub, False)

        @pl.when(jnp.logical_not(fit))
        def _():
            @pl.loop(0, per_step)
            def _(sub):
                forward(step * per_step + sub, True)

    hm_buf[...] = turned(node_w1[...])
    act_buf[:, :latent] = turned(node_w2[...])
    for blk in range(mesh_tiles // per_sub):
        tiles = range(blk * per_sub, (blk + 1) * per_sub)
        hm = jnp.concatenate([both_t[t, :latent] for t in tiles], axis=1)
        agg = jnp.concatenate([agg_buf[t].astype(BF) for t in tiles], axis=1)
        pre = mm(hm_buf[:, :latent], hm) + mm(hm_buf[:, latent:], agg) + col(3, 0)
        sig = sigmoid(pre)
        normed, _, inv = norm_fwd(mm(act_buf[:, :latent], (pre * sig).astype(BF)) + col(3, 1))
        out = (hm.astype(F32) + (normed * col(3, 2) + col(3, 3))).astype(BF)
        rows = pl.ds(blk * SUB, SUB)
        mesh_out[rows] = turned(out)
        g_two = norm_bwd(mm_t(eye, cot_ref[rows]) * col(3, 2), normed, inv).astype(BF)
        g_one = (mm(node_w2[...], g_two) * sig * (1.0 + pre * (1.0 - sig))).astype(BF)
        for idx, tile in enumerate(tiles):
            both_t[tile, latent:] = g_one[:, idx * LANES:(idx + 1) * LANES]

    @pl.loop(0, pairs)
    def _(step):
        fit = fit_ref[step] == 1

        @pl.when(fit)
        def _():
            for sub in range(per_step):
                backward(step * per_step + sub, False, sub)

        @pl.when(jnp.logical_not(fit))
        def _():
            @pl.loop(0, per_step)
            def _(sub):
                backward(step * per_step + sub, True, sub)

        w2_out[...] += mm_t(act_buf[...], g2_buf[...])
        g_one = g1_buf[...]
        span = pl.ds(pl.multiple_of(step * STEP, STEP), STEP)
        w1_out[:latent] += mm_t(he_buf[:, span], g_one)
        w1_out[2 * latent:] += mm_t(hm_buf[...], g_one)
        table_out[...] += mm_t(hot_buf[...], g_one)

    hi, mid, lo = split3(table_out[...])
    w1_out[latent:2 * latent] = mm(table_t[...], hi) + mm(table_t[...], mid) + mm(table_t[...], lo)
    w1b = w1[latent:2 * latent]
    table_out[...] = mm_t(hi, w1b) + mm_t(mid, w1b) + mm_t(lo, w1b)


def edge_call(first_tile, fits, live, feats, key_row, mesh_x, below, band, above, small_w, em_w2, mesh_w2, w1, w2,
              node_w1, node_w2, vecs, cot_mesh):
    latent = w2.shape[0]
    edges = key_row.shape[1]
    mesh_rows = cot_mesh.shape[0]
    mesh_tiles = mesh_rows // LANES
    table_rows = below.shape[0] + band.shape[0] + above.shape[0]
    vm = pl.BlockSpec(memory_space=pltpu.VMEM)
    sm = pl.BlockSpec(memory_space=pltpu.SMEM)
    scratch = [((latent, latent), BF), ((latent, 3 * latent), BF), ((latent, latent), BF), ((latent, table_rows), BF),
               ((mesh_tiles, 2 * latent, LANES), BF), ((8, latent, LANES), F32), ((latent, edges), F32), ((latent, edges), BF),
               ((1, edges), F32), ((1, edges), F32), ((mesh_tiles, latent, LANES), F32),
               ((latent, STEP), BF), ((latent, STEP), BF), ((latent, STEP), BF), ((latent, STEP), BF), ((table_rows, STEP), BF)]
    return pl.pallas_call(
        edge_kernel,
        in_specs=[sm] * 3 + [vm] * 15, out_specs=[vm] * 4,
        out_shape=[jax.ShapeDtypeStruct((mesh_rows, latent), BF), jax.ShapeDtypeStruct((3 * latent, latent), F32),
                   jax.ShapeDtypeStruct((latent, latent), F32), jax.ShapeDtypeStruct((table_rows, latent), F32)],
        scratch_shapes=[pltpu.VMEM(shape, dtype) for shape, dtype in scratch],
        compiler_params=pltpu.CompilerParams(vmem_limit_bytes=67043328),
        cost_estimate=pl.CostEstimate(flops=36 * edges * latent * latent, bytes_accessed=20 * 2 ** 20,
                                      transcendentals=3 * edges * latent),
        name="edge_both",
    )(first_tile, fits, live, feats, key_row, mesh_x, below, band, above, small_w, em_w2, mesh_w2, w1, w2,
      node_w1, node_w2, vecs, cot_mesh)


STRIDE = {'z': 32, 'y': 8, 'x': 2}
ORDERS = (('x', 'y', 'z'), ('y', 'z', 'x'), ('z', 'x', 'y'))
DIM = 4


def scatter_kernel(w1_ref, w2_ref, g1_out, g2_out, pair1, pair2, *scratch):
    full = scratch[0:3]
    recv = (scratch[3:6], scratch[6:9], scratch[9:12])
    part = (scratch[12:15], scratch[15:18])
    done1, done2, pair_send, pair_recv, hop_send, hop_recv = scratch[18:]
    me = lax.axis_index('graph')
    core = me % 2
    coord = {name: (me // stride) % DIM for name, stride in STRIDE.items()}
    partner = me + 1 - 2 * core

    def peer(name, hop):
        there = (coord[name] + hop) % DIM
        return there, me + (there - coord[name]) * STRIDE[name]

    barrier = pltpu.get_barrier_semaphore()
    others = [partner] + [peer(name, hop)[1] for name in STRIDE for hop in range(1, DIM)]
    for other in others:
        pl.semaphore_signal(barrier, inc=1, device_id={'graph': other}, device_id_type=MESH)
    pl.semaphore_wait(barrier, len(others))

    half = w1_ref.shape[-1] // 2
    mine = pl.multiple_of(core * half, half)
    theirs = pl.multiple_of((1 - core) * half, half)

    def to_partner(src, dst, slot):
        copy = pltpu.make_async_remote_copy(src_ref=src, dst_ref=dst, send_sem=pair_send.at[slot], recv_sem=pair_recv.at[slot],
                                            device_id={'graph': partner}, device_id_type=MESH)
        copy.start()
        return copy

    first = [to_partner(w1_ref.at[:, :, :, :, pl.ds(theirs, half)], pair1, 0),
             to_partner(w2_ref.at[:, :, :, :, pl.ds(theirs, half)], pair2, 1)]
    first[0].wait()
    quarter = half // 2
    full[0][...] = w1_ref[:, :, :, :, pl.ds(mine, quarter)] + pair1[:, :, :, :, :quarter]
    full[1][...] = w1_ref[:, :, :, :, pl.ds(mine + quarter, quarter)] + pair1[:, :, :, :, quarter:]
    first[1].wait()
    full[2][...] = w2_ref[:, :, :, :, pl.ds(mine, half)] + pair2[...]

    left = [list(STRIDE) for _ in range(3)]
    held = list(full)

    def at(color, name, index):
        pos = left[color].index(name)
        return (slice(None),) * pos + (index,)

    for stage in range(3):
        copies = []
        for color in range(3):
            name = ORDERS[color][stage]
            for hop in range(1, DIM):
                there, device = peer(name, hop)
                copy = pltpu.make_async_remote_copy(
                    src_ref=held[color].at[at(color, name, there)], dst_ref=recv[stage][color].at[hop - 1],
                    send_sem=hop_send.at[stage, color, hop - 1], recv_sem=hop_recv.at[stage, color, hop - 1],
                    device_id={'graph': device}, device_id_type=MESH)
                copy.start()
                copies.append(copy)
        for color in range(3):
            for copy in copies[3 * color:3 * color + 3]:
                copy.wait()
            name = ORDERS[color][stage]
            got = recv[stage][color]
            total = held[color][at(color, name, coord[name])] + got[0] + got[1] + got[2]
            left[color].remove(name)
            if stage < 2:
                part[stage][color][...] = total
                held[color] = part[stage][color]
            elif color == 2:
                done2[core] = total
            else:
                done1[core, :, color * quarter:(color + 1) * quarter] = total

    last = [to_partner(done1.at[core], done1.at[core], 2), to_partner(done2.at[core], done2.at[core], 3)]
    for copy in last:
        copy.wait()
    for done, out in ((done1, g1_out), (done2, g2_out)):
        rows = out.shape[0]
        whole = jnp.concatenate([done[0], done[1]], axis=1)
        out[...] = jnp.where(core == 0, whole[:rows], whole[rows:])


def scatter_call(w1, w2):
    rows1, rows2, cols = w1.shape[-2], w2.shape[-2], w1.shape[-1]
    half, quarter = cols // 2, cols // 4
    tail = ((rows1, quarter), (rows1, quarter), (rows2, half))
    scratch = [pltpu.VMEM((DIM,) * 3 + (rows1, half), F32), pltpu.VMEM((DIM,) * 3 + (rows2, half), F32)]
    scratch += [pltpu.VMEM((DIM,) * 3 + t, F32) for t in tail]
    for stage in range(3):
        scratch += [pltpu.VMEM((3,) + (DIM,) * (2 - stage) + t, F32) for t in tail]
    for stage in range(2):
        scratch += [pltpu.VMEM((DIM,) * (2 - stage) + t, F32) for t in tail]
    scratch += [pltpu.VMEM((2, rows1, half), F32), pltpu.VMEM((2, rows2, half), F32),
                pltpu.SemaphoreType.DMA((4,)), pltpu.SemaphoreType.DMA((4,)),
                pltpu.SemaphoreType.DMA((3, 3, 3)), pltpu.SemaphoreType.DMA((3, 3, 3))]
    vm = pl.BlockSpec(memory_space=pltpu.VMEM)
    return pl.pallas_call(
        scatter_kernel,
        in_specs=[vm, vm], out_specs=[vm, vm],
        out_shape=[jax.ShapeDtypeStruct((rows1 // 2, cols), F32), jax.ShapeDtypeStruct((rows2 // 2, cols), F32)],
        scratch_shapes=scratch,
        compiler_params=pltpu.CompilerParams(collective_id=0, has_side_effects=True, vmem_limit_bytes=40 * 2 ** 20),
        name="weight_scatter",
    )(w1, w2)


def mlp_forward(x_in, w_one, w_two, vec_rows):
    pre_one = jnp.dot(x_in, w_one, preferred_element_type=jnp.float32) + vec_rows[0]
    act_bf = jax.nn.silu(pre_one).astype(jnp.bfloat16)
    pre_two = jnp.dot(act_bf, w_two, preferred_element_type=jnp.float32) + vec_rows[1]
    centred = pre_two - jnp.mean(pre_two, axis=-1, keepdims=True)
    inv_std = lax.rsqrt(jnp.mean(centred * centred, axis=-1, keepdims=True) + NORM_EPS)
    normed = centred * inv_std
    return normed * vec_rows[2] + vec_rows[3], (pre_one, act_bf, normed, inv_std)


def mlp_backward(d_out, w_two, vec_rows, saved_acts):
    pre_one, act_bf, normed, inv_std = saved_acts
    d_norm = d_out * vec_rows[2]
    d_two = inv_std * (d_norm - jnp.mean(d_norm, axis=-1, keepdims=True)
                       - normed * jnp.mean(d_norm * normed, axis=-1, keepdims=True))
    g_two = d_two.astype(jnp.bfloat16)
    d_act = jnp.einsum('nj,kj->nk', g_two, w_two, preferred_element_type=jnp.float32)
    sig_pre = jax.nn.sigmoid(pre_one)
    d_one = d_act * sig_pre * (1.0 + pre_one * (1.0 - sig_pre))
    return d_one.astype(jnp.bfloat16), g_two


def solution(mesh):
    groups = mesh.shape['graph']
    row_spec = P(('batch', 'graph'), None)
    flat_spec = P(('batch', 'graph'))
    rep_spec = P(None, None)
    down_perm = [(src_dev, src_dev - 1) for src_dev in range(1, groups)]
    up_perm = [(src_dev, src_dev + 1) for src_dev in range(groups - 1)]

    def device_step(grid_in, mesh_in, edge_in, edge_src, edge_dst, edge_mask, grid_w1, grid_w2, grid_vec,
                    mesh_w1, mesh_w2, mesh_vec, embed_w1, embed_w2, embed_vec, edge_w1, edge_w2, edge_vec,
                    node_w1, node_w2, node_vec, post_w1, post_w2, post_vec, cot_mesh, cot_grid):
        band_rows = grid_in.shape[0]
        halo_rows = band_rows // 4
        latent = grid_w2.shape[1]
        mesh_rows = mesh_in.shape[0]
        edges = edge_in.shape[0]
        mesh_tiles = mesh_rows // LANES
        band_index = lax.axis_index('graph')

        grid_y, grid_saved = mlp_forward(grid_in.astype(BF), grid_w1, grid_w2, grid_vec)
        grid_h = grid_y.astype(BF)
        from_above = lax.ppermute(grid_h[:halo_rows], 'graph', down_perm)
        from_below = lax.ppermute(grid_h[band_rows - halo_rows:], 'graph', up_perm)

        local_src = edge_src - (band_index * band_rows - halo_rows)
        real = edge_mask != 0
        key = jnp.where(real, edge_dst * 2 ** KEY_BITS + local_src, mesh_rows * 2 ** KEY_BITS)
        feat_t = edge_in.T
        key, f0, f1, f2, f3 = lax.sort((key, feat_t[0], feat_t[1], feat_t[2], feat_t[3]), num_keys=1, is_stable=False)
        zero_row = jnp.zeros_like(f0)
        feats = jnp.stack([f0, f1, f2, f3, zero_row, zero_row, zero_row, zero_row])
        live = jnp.sum(real.astype(jnp.int32)).reshape(1)
        dst_sorted = (key >> KEY_BITS).reshape(-1, SUB)
        low = jnp.min(dst_sorted, axis=1)
        high = jnp.max(jnp.where(dst_sorted < mesh_rows, dst_sorted, 0), axis=1)
        first_tile = jnp.minimum(low // LANES, mesh_tiles - 2)
        fits = ((high - first_tile * LANES) < 2 * LANES).reshape(-1, STEP // SUB)
        fits = jnp.all(fits, axis=1).astype(jnp.int32)
        key_row = key.reshape(1, edges)
        mesh_x = jnp.pad(mesh_in.T, ((0, 8 - mesh_in.shape[1]), (0, 0)))
        small_w = jnp.concatenate([jnp.pad(embed_w1, ((0, 8 - embed_w1.shape[0]), (0, 0))),
                                   jnp.pad(mesh_w1, ((0, 8 - mesh_w1.shape[0]), (0, 0)))])
        vecs = jnp.concatenate([embed_vec, mesh_vec, edge_vec, node_vec])
        mesh_out, w1_part, w2_part, table_grad = edge_call(
            first_tile, fits, live, feats, key_row, mesh_x, from_below, grid_h, from_above, small_w, embed_w2, mesh_w2,
            edge_w1, edge_w2, node_w1, node_w2, vecs, cot_mesh)

        chips = (DIM, DIM, DIM)
        w1_grad, w2_grad = scatter_call(w1_part.reshape(chips + (-1, latent)), w2_part.reshape(chips + (-1, latent)))

        tail_grad = lax.ppermute(table_grad[:halo_rows], 'graph', down_perm)
        head_grad = lax.ppermute(table_grad[band_rows + halo_rows:], 'graph', up_perm)
        post_y, post_saved = mlp_forward(grid_h, post_w1, post_w2, post_vec)
        grid_out = (grid_h.astype(F32) + post_y).astype(BF)
        post_g1 = mlp_backward(cot_grid.astype(F32), post_w2, post_vec, post_saved)[0]
        grid_cot = cot_grid.astype(F32) + jnp.einsum('nj,kj->nk', post_g1, post_w1, preferred_element_type=F32)
        edge_part = table_grad[halo_rows:band_rows + halo_rows] + jnp.concatenate(
            [head_grad, jnp.zeros((band_rows - 2 * halo_rows, latent), F32), tail_grad], axis=0)
        grid_g1 = mlp_backward(grid_cot + edge_part, grid_w2, grid_vec, grid_saved)[0]
        grid_grad = jnp.einsum('nj,kj->nk', grid_g1, grid_w1, preferred_element_type=F32)
        return mesh_out, grid_out, grid_grad, w1_grad, w2_grad

    in_specs = (row_spec, row_spec, row_spec, flat_spec, flat_spec, flat_spec) + (rep_spec,) * 18 + (row_spec, row_spec)
    return jax.shard_map(device_step, mesh=mesh, in_specs=in_specs, out_specs=(row_spec,) * 5, check_vma=False)
```

time: 300 us -> 229 us (0.76)
  Pallas kernels: 188 us -> 139 us
  local copies, waits for them, and re-layouts: 35.9 us -> 9.43 us
  starting transfers between devices: 24.5 us -> 50.2 us
  matrix products: 23.1 us -> 11.2 us
  other arithmetic: 25 us -> 13.6 us
    pallas_call x2 -> x1, Pallas kernels: 138 us -> 89.6 us  [edge_call(): pl.pallas_call(edge_kernel, in_specs=[sm] * 3 + [vm] * 15, out_specs=[vm]...]
    ppermute x1, starting transfers between devices: 16.2 us -> 41.5 us  [device_step(): lax.ppermute(table_grad[band_rows + halo_rows:], 'graph', up_perm)]
    unnamed x94 -> x86, local copies, waits for them, and re-layouts: 15.5 us -> 4.99 us
    dot_general x4 -> x2, matrix products: 6.74 us -> 1.09 us  [mlp_forward(): jnp.dot(act_bf, w_two, preferred_element_type=jnp.float32) + vec_rows[1]]
    slice x5 -> x1, local copies, waits for them, and re-layouts: 5.11 us -> 0.02 us  [device_step(): from_above = lax.ppermute(grid_h[:halo_rows], 'graph', down_perm)]
    convert_element_type x2 -> x0, other arithmetic: 4.2 us -> none  [the longest x1 2.73 us: device_step(): agg_sum = jnp.swapaxes(agg_t, 1, 2).reshape(mesh_rows, latent).astype(BF)]
    dot_general x3 -> x2, matrix products: 6.19 us -> 2.02 us  [mlp_forward(): jnp.dot(x_in, w_one, preferred_element_type=jnp.float32) + vec_rows[0]]
    broadcast_in_dim x2 -> x0, local copies, waits for them, and re-layouts: 3.29 us -> none  [lane_table(): return jnp.broadcast_to(vec_rows[:, :, None], vec_rows.shape + (LANES,))]
  transfers between devices with their start and end apart: 4 -> 4, of which waited for: 0 -> 0; matrix products, arithmetic and copies ran while one was open for 14% -> 7% of each run, Pallas kernels for 17% -> 22%
where the time goes in v3:
time: 229 us; the launch traced here: 225 us
  Pallas kernels  139 us (61%)
  starting transfers between devices  50.2 us (22%)
  other arithmetic  13.6 us (6%)
  matrix products  11.2 us (5%)
  local copies, waits for them, and re-layouts  9.43 us (4%)
    pallas_call x1, Pallas kernels, edge_call(): pl.pallas_call(edge_kernel, in_specs=[sm] * 3 + [vm] * 15, out_specs=[vm]...  89.6 us
    pallas_call x1, Pallas kernels, scatter_call(): pl.pallas_call(scatter_kernel, in_specs=[vm, vm], out_specs=[vm, vm], out...  49.2 us
    ppermute x1, starting transfers between devices, device_step(): lax.ppermute(table_grad[band_rows + halo_rows:], 'graph', up_perm)  41.5 us
    sort x1, other arithmetic, device_step(): lax.sort((key, feat_t[0], feat_t[1], feat_t[2], feat_t[3]), num_keys=1, i...  5.85 us
    unnamed x86, local copies, waits for them, and re-layouts  4.99 us
    ppermute x1, starting transfers between devices, device_step(): from_below = lax.ppermute(grid_h[band_rows - halo_rows:], 'graph', up_perm)  4.63 us
  transfers between devices with their start and end apart: 4, of which 0 were waited for; matrix products, arithmetic and copies ran while one was open for 7% of the time, Pallas kernels for 22%

profile of v3, /device:TPU:1, one launch (start us, length us, event | category | flops | bytes accessed | tf_op | source)
XLA Modules:
  0.0 224.6 jit_solution(16390034750551728688)
XLA Ops:
  0.6 0.9 fusion.66
  1.5 1.6 convolution_add_fusion.4
  3.1 0.6 fusion.67
  3.7 0.4 copy-done.9
  4.1 0.0 copy-start.15
  4.2 0.3 multiply_reduce_fusion.2
  4.4 0.0 copy-start.10
  4.5 0.2 add_convert_fusion.1.band
  4.8 0.3 copy-done.2
  5.1 4.6 %collective-permute-start = (bf16[128,512]{1,0:T(8,128)(2,1)S(1)}, bf16[128,512]{1,0:T(8,128)(2,1)S(1)}, u32[]{:S(2)}, u32[]{:S(2)}) collective-permute-start(bf16[128,512]{1,0:T(8,128)(2,1)S(1)} %get-tuple-element.39), channel_id=1, source_target_pairs={{0,1},{1,2},{2,3},{3,4},{4,5},{5,6},{6,7},{7,8},{8,9},{9,10},{10,1... | collective-permute-start | bytes 393224 | tf_op jit(solution)/shard_map/ppermute | solution.py:396
  9.8 1.9 collective-permute-start.1
  11.7 0.1 fusion.64
  11.8 0.6 convert_reduce_fusion
  12.5 5.9 %sort.33 = (s32[8192]{0:T(1024)S(1)}, f32[8192]{0:T(1024)S(1)}, f32[8192]{0:T(1024)S(1)}, f32[8192]{0:T(1024)S(1)}, f32[8192]{0:T(1024)S(1)}) sort(s32[8192]{0:T(1024)S(1)} %add_select_fusion, f32[8192]{0:T(1024)S(1)} %bitcast.37, f32[8192]{0:T(1024)S(1)} %bitcast.36, f32[8192]{0:T(1024)S(1)} %bitcast.35, f32[8192]{0:T(1024)S(1)} %bitcast.34), dimensions={0}, to_apply=%region_0.1 | sort | flops 106496 | bytes 327680 | tf_op jit(solution)/shard_map/sort | solution.py:402
  18.4 0.1 fusion.45
  18.5 0.1 reduce_min.12
  18.6 0.5 fusion.56.first_ref
  19.1 0.1 reduce_max.12
  19.2 0.6 fusion.65
  19.8 0.4 convolution_add_fusion.2
  20.2 0.0 copy-start.34
  20.2 0.0 copy-start.35
  20.3 0.5 fusion.68
  20.8 0.4 copy-done.7
  21.2 1.0 copy-done.4
  22.2 0.3 multiply_reduce_fusion.1
  22.5 0.6 add_rsqrt_fusion
  23.0 0.1 fusion.55
  23.2 0.6 fusion.48.small_w
  23.8 0.5 convert_element_type.46.fit_ref
  24.3 0.6 pad.12.mesh_x
  24.9 0.9 stack.23.feat_ref
  25.9 0.6 pad_maximum_fusion.vecs
  26.5 0.6 copy-done.40
  27.2 0.1 copy-done.41
  27.2 89.6 %edge_both.1 = (bf16[1024,512]{1,0:T(8,128)(2,1)}, f32[1536,512]{1,0:T(8,128)}, f32[512,512]{1,0:T(8,128)}, f32[768,512]{1,0:T(8,128)}) custom-call(s32[16]{0:T(128)} %fusion.56.first_ref, s32[8]{0:T(128)} %convert_element_type.46.fit_ref, s32[1]{0:T(128)} %bitcast.5.live_ref, f32[8,8192]{1,0:T(8,128)} %stack.23.feat_ref, s32[1,8192]{1,0:T(1,128)} %bitcast.42, ...), custom_call_target="tpu_custom_call" | custom-call | flops 77309411328 | bytes 20971520 | tf_op jit(solution)/shard_map/edge_both/pallas_call | solution.py:227
  116.8 1.2 fusion.62
  118.0 41.5 %collective-permute-start.2 = (f32[128,512]{1,0:T(8,128)S(1)}, f32[128,512]{1,0:T(8,128)S(1)}, u32[]{:S(2)}, u32[]{:S(2)}) collective-permute-start(f32[128,512]{1,0:T(8,128)S(1)} %get-tuple-element.35), channel_id=1, source_target_pairs={{0,1},{1,2},{2,3},{3,4},{4,5},{5,6},{6,7},{7,8},{8,9},{9,10},{10,1... | collective-permute-start | bytes 786440 | tf_op jit(solution)/shard_map/ppermute | solution.py:425
  159.5 2.1 collective-permute-start.3
  161.6 3.3 %fusion.4 = (f32[512]{0:T(512)S(1)}, f32[512]{0:T(512)S(1)}, bf16[512,512]{1,0:T(8,128)(2,1)}) fusion(bf16[512,512]{1,0:T(8,128)(2,1)} %param.51, f32[512]{0:T(512)} %bitcast.49, f32[512]{0:T(512)} %add_rsqrt_fusion, f32[512,512]{1,0:T(8,128)} %copy-done.4, f32[512]{0:T(512)} %copy-done.21, f32[512]{0:T(512)} %bitcast.51, f32[512]{0:T(512)} %bitcast.47, ...), kind=kLoop, calls=%fused_computation.12 | loop fusion | flops 4455424 | bytes 3166208 | tf_op jit(solution)/shard_map/reduce_sum | solution.py:365
  165.0 0.0 copy-start.28
  165.0 49.2 %weight_scatter.1 = (f32[12,512]{1,0:T(8,128)S(1)}, f32[4,512]{1,0:T(4,128)S(1)}) custom-call(f32[4,4,4,24,512]{4,3,2,1,0:T(8,128)S(1)} %bitcast.31, f32[4,4,4,8,512]{4,3,2,1,0:T(8,128)S(1)} %bitcast.32), custom_call_target="tpu_custom_call" | custom-call | tf_op jit(solution)/shard_map/weight_scatter/pallas_call | solution.py:342
  214.3 0.7 copy-done.38
  215.0 0.1 copy-done.39
  215.1 4.5 %fusion.61 = (f32[512]{0:T(512)S(1)}, f32[512]{0:T(512)S(1)}, f32[512,512]{1,0:T(8,128)}) fusion(f32[512]{0:T(512)S(1)} %copy-done.20, f32[512,512]{1,0:T(8,128)S(1)} %copy-done.3, f32[512]{0:T(512)S(1)} %copy-done.14, f32[512]{0:T(512)S(1)} %bitcast.45, f32[128,512]{1,0:T(8,128)} %copy-done.39, f32[512]{0:T(512)S(1)} %pad.16.clone, ...), kind=kOutput, calls=%fused_computation.96 | convolution fusion | flops 544734208 | bytes 7886848 | tf_op jit(solution)/shard_map/nj,kj->nk/dot_general | solution.py:429
  219.6 3.6 %fusion.7 = f32[512,267]{0,1:T(8,128)} fusion(bf16[267,512]{1,0:T(8,128)(2,1)S(1)} %copy-done.11, bf16[512,512]{1,0:T(8,128)(2,1)} %param.33, f32[512,512]{1,0:T(8,128)} %copy-done.9, f32[512,512]{1,0:T(8,128)} %get-tuple-element.56, f32[512,512]{1,0:T(8,128)S(1)} %copy-done.3, f32[512]{0:T(512)S(1)} %broadcast_multiply_fusion, ...), kind=kOutput, calls=%fused_computation.15 | convolution fusion | flops 412614656 | bytes 4498432 | tf_op jit(solution)/shard_map/nj,kj->nk/dot_general | solution.py:433
  223.2 0.6 copy.45
  223.8 0.6 copy.46
  (88 shorter events, 0.3 us)
Async XLA Ops:
  0.6 2.5 %copy-start.37 = (bf16[512,512]{1,0:T(8,128)(2,1)S(1)}, bf16[512,512]{1,0:T(8,128)(2,1)}, u32[]{:S(2)}) copy-start(bf16[512,512]{1,0:T(8,128)(2,1)} %param.33) | copy-start | bytes 1572868
  1.5 3.0 %copy-start.23 = (f32[1,512]{1,0:T(1,128)}, f32[1,512]{1,0:T(1,128)S(1)}, u32[]{:S(2)}) copy-start(f32[1,512]{1,0:T(1,128)S(1)} %get-tuple-element.48) | copy-start | bytes 6148
  1.5 3.0 %copy-start.25 = (f32[1,512]{1,0:T(1,128)}, f32[1,512]{1,0:T(1,128)S(1)}, u32[]{:S(2)}) copy-start(f32[1,512]{1,0:T(1,128)S(1)} %get-tuple-element.51) | copy-start | bytes 6148
  3.1 1.0 copy-start.9
  4.1 1.0 copy-start.2
  4.1 1.0 copy-start.13
  4.1 7.6 %copy-start.12 = (f32[8192,4]{0,1:T(4,128)S(1)}, f32[8192,4]{0,1:T(4,128)}, u32[]{:S(2)}) copy-start(f32[8192,4]{0,1:T(4,128)} %param.28) | copy-start | bytes 393220
  4.1 7.7 %copy-start.15 = (s32[8192]{0:T(1024)S(1)}, s32[8192]{0:T(1024)}, u32[]{:S(2)}) copy-start(s32[8192]{0:T(1024)} %param.31) | copy-start | bytes 98308
  4.2 8.3 %copy-start.16 = (s32[8192]{0:T(1024)S(1)}, s32[8192]{0:T(1024)}, u32[]{:S(2)}) copy-start(s32[8192]{0:T(1024)} %param.29) | copy-start | bytes 98308
  4.2 8.3 %copy-start.17 = (s32[8192]{0:T(1024)S(1)}, s32[8192]{0:T(1024)}, u32[]{:S(2)}) copy-start(s32[8192]{0:T(1024)} %param.30) | copy-start | bytes 98308
  4.4 14.7 %copy-start.29 = (f32[4,512]{1,0:T(4,128)S(1)}, f32[4,512]{1,0:T(4,128)}, u32[]{:S(2)}) copy-start(f32[4,512]{1,0:T(4,128)} %param.49) | copy-start | bytes 24580
  4.4 15.3 %copy-start.10 = (bf16[512,512]{1,0:T(8,128)(2,1)S(1)}, bf16[512,512]{1,0:T(8,128)(2,1)}, u32[]{:S(2)}) copy-start(bf16[512,512]{1,0:T(8,128)(2,1)} %param.47) | copy-start | bytes 1572868
  4.5 7.2 %copy-start.19 = (f32[512]{0:T(512)}, f32[512]{0:T(512)S(1)}, u32[]{:S(2)}) copy-start(f32[512]{0:T(512)S(1)} %add_rsqrt_fusion.1) | copy-start | bytes 6148
  4.7 15.5 %copy-start.6 = (bf16[512,512]{1,0:T(8,128)(2,1)}, bf16[512,512]{1,0:T(8,128)(2,1)S(1)}, u32[]{:S(2)}) copy-start(bf16[512,512]{1,0:T(8,128)(2,1)S(1)} %add_convert_fusion.1.band) | copy-start | bytes 1572868
  5.1 15.1 %copy-start.36 = (bf16[512,512]{1,0:T(8,128)(2,1)S(1)}, bf16[512,512]{1,0:T(8,128)(2,1)}, u32[]{:S(2)}) copy-start(bf16[512,512]{1,0:T(8,128)(2,1)} %param.48) | copy-start | bytes 1572868
  5.1 21.4 %collective-permute-start = (bf16[128,512]{1,0:T(8,128)(2,1)S(1)}, bf16[128,512]{1,0:T(8,128)(2,1)S(1)}, u32[]{:S(2)}, u32[]{:S(2)}) collective-permute-start(bf16[128,512]{1,0:T(8,128)(2,1)S(1)} %get-tuple-element.39), channel_id=1, source_target_pairs={{0,1},{1,2},{2,3},{3,4},{4,5},{5,6},{6,7},{7,8},{8,9},{9,10},{10,1... | collective-permute-start | bytes 393224 | tf_op jit(solution)/shard_map/ppermute | solution.py:396
  9.8 16.8 %collective-permute-start.1 = (bf16[128,512]{1,0:T(8,128)(2,1)S(1)}, bf16[128,512]{1,0:T(8,128)(2,1)S(1)}, u32[]{:S(2)}, u32[]{:S(2)}) collective-permute-start(bf16[128,512]{1,0:T(8,128)(2,1)S(1)} %get-tuple-element.38), channel_id=1, source_target_pairs={{1,0},{2,1},{3,2},{4,3},{5,4},{6,5},{7,6},{8,7},{9,8},{10,9},{11,1... | collective-permute-start | bytes 393224 | tf_op jit(solution)/shard_map/ppermute | solution.py:395
  18.3 2.5 %copy-start.18 = (s32[8192]{0:T(1024)}, s32[8192]{0:T(1024)S(1)}, u32[]{:S(2)}) copy-start(s32[8192]{0:T(1024)S(1)} %get-tuple-element.16) | copy-start | bytes 98308
  20.2 1.0 copy-start.7
  20.2 2.9 %copy-start.34 = (bf16[3,512]{1,0:T(4,128)(2,1)S(1)}, bf16[3,512]{1,0:T(4,128)(2,1)}, u32[]{:S(2)}) copy-start(bf16[3,512]{1,0:T(4,128)(2,1)} %param.35) | copy-start | bytes 9220
  20.2 2.9 %copy-start.35 = (bf16[4,512]{1,0:T(4,128)(2,1)S(1)}, bf16[4,512]{1,0:T(4,128)(2,1)}, u32[]{:S(2)}) copy-start(bf16[4,512]{1,0:T(4,128)(2,1)} %param.38) | copy-start | bytes 12292
  20.2 4.1 %copy-start.26 = (f32[1024,3]{0,1:T(4,128)S(1)}, f32[1024,3]{0,1:T(4,128)}, u32[]{:S(2)}) copy-start(f32[1024,3]{0,1:T(4,128)} %param.27) | copy-start | bytes 36868
  21.2 1.0 copy-start.4
  21.2 4.7 %copy-start.30 = (f32[4,512]{1,0:T(4,128)S(1)}, f32[4,512]{1,0:T(4,128)}, u32[]{:S(2)}) copy-start(f32[4,512]{1,0:T(4,128)} %param.46) | copy-start | bytes 24580
  21.2 4.7 %copy-start.31 = (f32[4,512]{1,0:T(4,128)S(1)}, f32[4,512]{1,0:T(4,128)}, u32[]{:S(2)}) copy-start(f32[4,512]{1,0:T(4,128)} %param.43) | copy-start | bytes 24580
  21.2 4.7 %copy-start.32 = (f32[4,512]{1,0:T(4,128)S(1)}, f32[4,512]{1,0:T(4,128)}, u32[]{:S(2)}) copy-start(f32[4,512]{1,0:T(4,128)} %param.37) | copy-start | bytes 24580
  21.2 4.7 %copy-start.33 = (f32[4,512]{1,0:T(4,128)S(1)}, f32[4,512]{1,0:T(4,128)}, u32[]{:S(2)}) copy-start(f32[4,512]{1,0:T(4,128)} %param.40) | copy-start | bytes 24580
  21.2 5.3 %copy-start.21 = (f32[512]{0:T(512)}, f32[512]{0:T(512)S(1)}, u32[]{:S(2)}) copy-start(f32[512]{0:T(512)S(1)} %broadcast_multiply_fusion.4) | copy-start | bytes 6148
  26.5 0.6 copy-start.40
  26.5 0.7 copy-start.41
  116.8 48.1 %copy-start.1 = (f32[512,512]{1,0:T(8,128)S(1)}, f32[512,512]{1,0:T(8,128)}, u32[]{:S(2)}) copy-start(f32[512,512]{1,0:T(8,128)} %get-tuple-element.24) | copy-start | bytes 3145732
  118.0 96.3 %collective-permute-start.2 = (f32[128,512]{1,0:T(8,128)S(1)}, f32[128,512]{1,0:T(8,128)S(1)}, u32[]{:S(2)}, u32[]{:S(2)}) collective-permute-start(f32[128,512]{1,0:T(8,128)S(1)} %get-tuple-element.35), channel_id=1, source_target_pairs={{0,1},{1,2},{2,3},{3,4},{4,5},{5,6},{6,7},{7,8},{8,9},{9,10},{10,1... | collective-permute-start | bytes 786440 | tf_op jit(solution)/shard_map/ppermute | solution.py:425
  159.5 54.8 %collective-permute-start.3 = (f32[128,512]{1,0:T(8,128)S(1)}, f32[128,512]{1,0:T(8,128)S(1)}, u32[]{:S(2)}, u32[]{:S(2)}) collective-permute-start(f32[128,512]{1,0:T(8,128)S(1)} %get-tuple-element.36), channel_id=1, source_target_pairs={{1,0},{2,1},{3,2},{4,3},{5,4},{6,5},{7,6},{8,7},{9,8},{10,9},{11,1... | collective-permute-start | bytes 786440 | tf_op jit(solution)/shard_map/ppermute | solution.py:424
  161.6 3.3 %copy-start = (f32[1536,512]{1,0:T(8,128)S(1)}, f32[1536,512]{1,0:T(8,128)}, u32[]{:S(2)}) copy-start(f32[1536,512]{1,0:T(8,128)} %get-tuple-element.23) | copy-start | bytes 9437188
  164.9 50.1 %copy-start.3 = (f32[512,512]{1,0:T(8,128)S(1)}, f32[512,512]{1,0:T(8,128)}, u32[]{:S(2)}) copy-start(f32[512,512]{1,0:T(8,128)} %copy-done.2) | copy-start | bytes 3145732
  164.9 50.1 %copy-start.5 = (f32[512,512]{1,0:T(8,128)S(1)}, f32[512,512]{1,0:T(8,128)}, u32[]{:S(2)}) copy-start(f32[512,512]{1,0:T(8,128)} %copy-done.4) | copy-start | bytes 3145732
  165.0 50.1 %copy-start.8 = (f32[512,512]{1,0:T(8,128)S(1)}, f32[512,512]{1,0:T(8,128)}, u32[]{:S(2)}) copy-start(f32[512,512]{1,0:T(8,128)} %copy-done.7) | copy-start | bytes 3145732
  165.0 50.1 %copy-start.14 = (f32[512]{0:T(512)S(1)}, f32[512]{0:T(512)}, u32[]{:S(2)}) copy-start(f32[512]{0:T(512)} %copy-done.13) | copy-start | bytes 6148
  165.0 50.1 %copy-start.20 = (f32[512]{0:T(512)S(1)}, f32[512]{0:T(512)}, u32[]{:S(2)}) copy-start(f32[512]{0:T(512)} %copy-done.19) | copy-start | bytes 6148
  165.0 50.1 %copy-start.22 = (f32[512]{0:T(512)S(1)}, f32[512]{0:T(512)}, u32[]{:S(2)}) copy-start(f32[512]{0:T(512)} %copy-done.21) | copy-start | bytes 6148
  165.0 50.1 %copy-start.24 = (f32[1,512]{1,0:T(1,128)S(1)}, f32[1,512]{1,0:T(1,128)}, u32[]{:S(2)}) copy-start(f32[1,512]{1,0:T(1,128)} %copy-done.23) | copy-start | bytes 6148
  165.0 50.1 %copy-start.27 = (f32[512]{0:T(512)S(1)}, f32[512]{0:T(512)}, u32[]{:S(2)}) copy-start(f32[512]{0:T(512)} %add_rsqrt_fusion) | copy-start | bytes 6148
  165.0 50.1 %copy-start.28 = (f32[1,512]{1,0:T(1,128)S(1)}, f32[1,512]{1,0:T(1,128)}, u32[]{:S(2)}) copy-start(f32[1,512]{1,0:T(1,128)} %get-tuple-element.44) | copy-start | bytes 6148
  214.2 0.7 copy-start.38
  214.3 0.8 copy-start.39
  215.1 4.5 %copy-start.11 = (bf16[267,512]{1,0:T(8,128)(2,1)S(1)}, bf16[267,512]{1,0:T(8,128)(2,1)}, u32[]{:S(2)}) copy-start(bf16[267,512]{1,0:T(8,128)(2,1)} %param.32) | copy-start | bytes 820228
